TPU v7x, 256 devices: a whole 4x4x8 slice. The times are simulated.
256 devices in a mesh: tm: 8 (over y, core), space: 32 (over z, x).
Axes of the slice: x: 4, y: 4, z: 8, core: 2. Of those that a mesh axis runs over, the one named last changes fastest.
Arguments:
- state: bfloat16 [8, 16384, 137], P('tm', 'space'), may hold values from -6 to 6
- obs_start: int32 [131072], P(('tm', 'space')), may hold values from 0 to 16383, as said below
- foot_weight: bfloat16 [131072, 8], P(('tm', 'space')), may hold values from 0.019897461 to 0.29882812
- obs_slot: int32 [131072], P(('tm', 'space')), may hold values from 0 to 6
- obs_frac: float32 [131072], P(('tm', 'space')), may hold values from 0 to 1
- live_count: int32 [8, 32], P('tm', 'space'), may hold values from 64 to 512
- obs_values: float32 [131072, 128], P(('tm', 'space')), may hold values from -6 to 6
- jacobian: bfloat16 [137, 128], replicated, may hold values from -0.5 to 0.5
- inv_var: float32 [128], replicated, may hold values from 0.25 to 4
Outputs:
- departures: float32 [131072, 128], P(('tm', 'space'))
- adjoint: float32 [8, 16384, 137], P('tm', 'space')
Inputs may be any that keep to these rules, and one draw needn't show every extreme that they name: `obs_start`: on the devices of space index s, every observation's footprint columns lie within 256 columns of tile s, that is within s * 512 - 256 .. (s + 1) * 512 + 255 taken modulo 16384. `live_count`: rows at or beyond a device's count are padding.
All inputs are finite; a program needn't handle non-finite values.
Results may differ from a plain program's by a relative error of at most 0.008.
Values may be sent and summed in bfloat16 or wider, within the bound.
A program may use at most 64 MiB of HBM per device.

v0:
```python
import jax
import jax.numpy as jnp
from jax import lax
from jax.sharding import PartitionSpec as P

block_rows = 128


def with_halo(cells, sides, width):
    for axis, dim in sides:
        count = lax.axis_size(axis)
        head = lax.slice_in_dim(cells, 0, width, axis=dim)
        tail = lax.slice_in_dim(cells, cells.shape[dim] - width, cells.shape[dim], axis=dim)
        cells = jnp.concatenate(
            [
                lax.ppermute(tail, axis, [(i, (i + 1) % count) for i in range(count)]),
                cells,
                lax.ppermute(head, axis, [((i + 1) % count, i) for i in range(count)]),
            ],
            axis=dim,
        )
    return cells


def shifted(block, axis, distance):
    devices = range(lax.axis_size(axis))
    route = [((i - distance) % len(devices), i) for i in devices]
    return lax.ppermute(block, axis, route)


def footprint_matrix(starts, weights, tile, cols_dev, halo_w, total_cols):
    local = jnp.mod(starts - tile * cols_dev + halo_w, total_cols)
    width = cols_dev + 2 * halo_w
    place = lax.broadcasted_iota(jnp.int32, (starts.shape[0], width), 1)
    offset = place - local[:, None]
    matrix = jnp.zeros((starts.shape[0], width), jnp.float32)
    for column in range(weights.shape[1]):
        matrix = matrix + jnp.where(
            offset == column, weights[:, column : column + 1].astype(jnp.float32), 0.0
        )
    return matrix.astype(jnp.bfloat16)


def time_weight(slot, frac, held):
    return jnp.where(slot == held, 1.0 - frac, 0.0) + jnp.where(slot + 1 == held, frac, 0.0)


def gather_slot(interp, foot_mat, wide, weight, blocks):

    def gather_one_block(index, total):
        first = index * block_rows
        rows = lax.dynamic_slice_in_dim(foot_mat, first, block_rows, 0)
        part = jnp.dot(rows, wide, preferred_element_type=jnp.float32)
        scale = lax.dynamic_slice_in_dim(weight, first, block_rows, 0)
        current = lax.dynamic_slice_in_dim(total, first, block_rows, 0)
        return lax.dynamic_update_slice_in_dim(total, current + scale[:, None] * part, first, 0)

    return lax.fori_loop(0, blocks, gather_one_block, interp)


def spread_slot(foot_mat, back, weight, blocks, width, levels):

    def spread_one_block(index, total):
        first = index * block_rows
        rows = lax.dynamic_slice_in_dim(foot_mat, first, block_rows, 0)
        scale = lax.dynamic_slice_in_dim(weight, first, block_rows, 0)
        source = lax.dynamic_slice_in_dim(back, first, block_rows, 0)
        part = (scale[:, None] * source.astype(jnp.float32)).astype(jnp.bfloat16)
        return total + lax.dot_general(
            rows, part, (((0,), (0,)), ((), ())), preferred_element_type=jnp.float32
        )

    return lax.fori_loop(0, blocks, spread_one_block, jnp.zeros((width, levels), jnp.float32))


def fold_rims(wide, from_left, from_right, halo_w, cols_dev):
    core = wide[halo_w : halo_w + cols_dev]
    core = core.at[:halo_w].add(from_left)
    return core.at[cols_dev - halo_w :].add(from_right)


def body(
    state, obs_start, foot_weight, obs_slot, obs_frac, live_count, obs_values, jacobian, inv_var
):
    own = state[0]
    cols_dev, levels = own.shape
    halo_w = cols_dev // 2
    width = cols_dev + 2 * halo_w
    slots = lax.axis_size("tm")
    tile = lax.axis_index("space")
    turn = lax.axis_index("tm")
    total_cols = cols_dev * lax.axis_size("space")
    count = live_count[0, 0]
    blocks = (count + block_rows - 1) // block_rows
    obs_rows = obs_start.shape[0]
    foot_mat = footprint_matrix(obs_start, foot_weight, tile, cols_dev, halo_w, total_cols)
    interp = jnp.zeros((obs_rows, levels), jnp.float32)

    def forward_weight(step):
        return time_weight(obs_slot, obs_frac, jnp.mod(turn - step, slots))

    def backward_weight(step):
        return time_weight(obs_slot, obs_frac, jnp.mod(turn + slots - 1 - step, slots))

    wide_own = with_halo(own, (("space", 0),), halo_w)
    interp = gather_slot(interp, foot_mat, wide_own, forward_weight(0), blocks)

    def forward_wide(step, carry):
        wide, total = carry
        wide = shifted(wide, "tm", 1)
        return (wide, gather_slot(total, foot_mat, wide, forward_weight(step), blocks))

    carried, interp = lax.fori_loop(1, slots, forward_wide, (wide_own, interp))
    projected = jnp.dot(interp.astype(jnp.bfloat16), jacobian, preferred_element_type=jnp.float32)
    row_live = jnp.arange(obs_rows, dtype=jnp.int32) < count
    departures = jnp.where(row_live[:, None], obs_values - projected, 0.0)
    scaled = (departures * inv_var[None, :]).astype(jnp.bfloat16)
    back = jnp.dot(scaled, jacobian.T, preferred_element_type=jnp.float32).astype(jnp.bfloat16)

    def backward_wide(step, total):
        total = shifted(total.astype(jnp.bfloat16), "tm", 1).astype(total.dtype)
        return total + spread_slot(foot_mat, back, backward_weight(step), blocks, width, levels)

    start_sum = spread_slot(foot_mat, back, backward_weight(0), blocks, width, levels)
    wide_sum = lax.fori_loop(1, slots, backward_wide, start_sum)
    from_right = shifted(wide_sum[:halo_w], "space", -1)
    from_left = shifted(wide_sum[halo_w + cols_dev :], "space", 1)
    adjoint = fold_rims(wide_sum, from_left, from_right, halo_w, cols_dev)
    return (departures, adjoint[None])


def solution(mesh):
    return jax.shard_map(
        body,
        mesh=mesh,
        in_specs=(
            P("tm", "space", None),
            P(("tm", "space")),
            P(("tm", "space"), None),
            P(("tm", "space")),
            P(("tm", "space")),
            P("tm", "space"),
            P(("tm", "space"), None),
            P(),
            P(),
        ),
        out_specs=(P(("tm", "space"), None), P("tm", "space", None)),
        check_vma=False,
    )
```

profile of v0, /device:TPU:102, one launch (start us, length us, event | category | flops | bytes accessed | tf_op | source)
XLA Modules:
  0.0 165.7 jit_solution(18098735830261789659)
XLA Ops:
  1.8 3.1 %collective-permute-start.2 = (bf16[256,137]{1,0:T(8,128)(2,1)S(1)}, bf16[256,137]{1,0:T(8,128)(2,1)S(1)}, u32[]{:S(2)}, u32[]{:S(2)}) collective-permute-start(bf16[256,137]{1,0:T(8,128)(2,1)S(1)} %get-tuple-element.793), channel_id=1, source_target_pairs={{0,1},{1,2},{2,3},{3,4},{4,5},{5,6},{6,7},{7,8},{8,9},{9,10},{10,1... | collective-permute-start | bytes 210440 | tf_op jit(solution)/shard_map/ppermute | solution.py:16
  6.7 1.9 %add_convert_fusion.2 = bf16[512,1024]{1,0:T(8,128)(2,1)S(1)} fusion(f32[512]{0:T(512)S(1)} %bitcast.40, f32[512]{0:T(512)S(1)} %bitcast.42, f32[512]{0:T(512)S(1)} %bitcast.30, f32[512]{0:T(512)S(1)} %bitcast.32, f32[512]{0:T(512)S(1)} %bitcast.34, f32[512]{0:T(512)S(1)} %bitcast.36, f32[512]{0:T(512)S(1)} %bitcast.38, f32[512]{0:T(512)S(1)} %bitcast.28, ...), kind=kLoop, calls=%fused_computation.49 | loop fusion | flops 13107200 | bytes 1067008 | tf_op jit(solution)/shard_map/convert_element_type | solution.py:41
  8.6 4.6 %collective-permute-done.3 = bf16[256,137]{1,0:T(8,128)(2,1)S(1)} collective-permute-done((bf16[256,137]{1,0:T(8,128)(2,1)S(1)}, bf16[256,137]{1,0:T(8,128)(2,1)S(1)}, u32[]{:S(2)}, u32[]{:S(2)}) %collective-permute-start.3) | collective-permute-done | bytes 70176 | tf_op jit(solution)/shard_map/ppermute | solution.py:18
  13.3 1.6 while.115
  15.9 80.3 %while.118 = (s32[]{:T(128)}, bf16[1024,137]{1,0:T(8,128)(2,1)S(1)}, f32[512,137]{0,1:T(8,128)S(1)}, s32[]{:T(128)}, s32[512]{0:T(512)S(1)}, /*index=5*/f32[512]...) while((s32[]{:T(128)}, bf16[1024,137]{1,0:T(8,128)(2,1)S(1)}, ...), condition=%wide.region_5.6_spmd.clone, body=%wide.region_2.5_spmd.clone.sunk | while | flops 49059600 | bytes 3693673 | solution.py:113
  15.9 1.8 %add_convert_fusion.5 = bf16[512,1024]{1,0:T(8,128)(2,1)S(1)} fusion(f32[512]{0:T(512)S(1)} %get-tuple-element.1334, f32[512]{0:T(512)S(1)} %get-tuple-element.1332, f32[512]{0:T(512)S(1)} %get-tuple-element.1331, f32[512]{0:T(512)S(1)} %get-tuple-element.1330, f32[512]{0:T(512)S(1)} %get-tuple-element.1329, f32[512]{0:T(512)S(1)} %get-tuple-element.1328, ...), kind=kLoop, calls=%fused_computation.24.clone.1 | loop fusion | flops 13107200 | bytes 1067008 | tf_op jit(solution)/shard_map/convert_element_type | solution.py:41
  17.8 7.9 %collective-permute-done.1 = bf16[1024,137]{1,0:T(8,128)(2,1)S(1)} collective-permute-done((bf16[1024,137]{1,0:T(8,128)(2,1)S(1)}, bf16[1024,137]{1,0:T(8,128)(2,1)S(1)}, u32[]{:S(2)}, u32[]{:S(2)}) %collective-permute-start.1) | collective-permute-done | bytes 280608 | tf_op jit(solution)/shard_map/while/body/eval_jaxpr/ppermute | solution.py:28
  25.7 1.6 while.121
  27.4 1.9 %add_convert_fusion.5 = bf16[512,1024]{1,0:T(8,128)(2,1)S(1)} fusion(f32[512]{0:T(512)S(1)} %get-tuple-element.1334, f32[512]{0:T(512)S(1)} %get-tuple-element.1332, f32[512]{0:T(512)S(1)} %get-tuple-element.1331, f32[512]{0:T(512)S(1)} %get-tuple-element.1330, f32[512]{0:T(512)S(1)} %get-tuple-element.1329, f32[512]{0:T(512)S(1)} %get-tuple-element.1328, ...), kind=kLoop, calls=%fused_computation.24.clone.1 | loop fusion | flops 13107200 | bytes 1067008 | tf_op jit(solution)/shard_map/convert_element_type | solution.py:41
  29.3 7.9 %collective-permute-done.1 = bf16[1024,137]{1,0:T(8,128)(2,1)S(1)} collective-permute-done((bf16[1024,137]{1,0:T(8,128)(2,1)S(1)}, bf16[1024,137]{1,0:T(8,128)(2,1)S(1)}, u32[]{:S(2)}, u32[]{:S(2)}) %collective-permute-start.1) | collective-permute-done | bytes 280608 | tf_op jit(solution)/shard_map/while/body/eval_jaxpr/ppermute | solution.py:28
  37.2 1.6 while.121
  38.9 1.9 %add_convert_fusion.5 = bf16[512,1024]{1,0:T(8,128)(2,1)S(1)} fusion(f32[512]{0:T(512)S(1)} %get-tuple-element.1334, f32[512]{0:T(512)S(1)} %get-tuple-element.1332, f32[512]{0:T(512)S(1)} %get-tuple-element.1331, f32[512]{0:T(512)S(1)} %get-tuple-element.1330, f32[512]{0:T(512)S(1)} %get-tuple-element.1329, f32[512]{0:T(512)S(1)} %get-tuple-element.1328, ...), kind=kLoop, calls=%fused_computation.24.clone.1 | loop fusion | flops 13107200 | bytes 1067008 | tf_op jit(solution)/shard_map/convert_element_type | solution.py:41
  40.8 7.9 %collective-permute-done.1 = bf16[1024,137]{1,0:T(8,128)(2,1)S(1)} collective-permute-done((bf16[1024,137]{1,0:T(8,128)(2,1)S(1)}, bf16[1024,137]{1,0:T(8,128)(2,1)S(1)}, u32[]{:S(2)}, u32[]{:S(2)}) %collective-permute-start.1) | collective-permute-done | bytes 280608 | tf_op jit(solution)/shard_map/while/body/eval_jaxpr/ppermute | solution.py:28
  50.4 1.9 %add_convert_fusion.5 = bf16[512,1024]{1,0:T(8,128)(2,1)S(1)} fusion(f32[512]{0:T(512)S(1)} %get-tuple-element.1334, f32[512]{0:T(512)S(1)} %get-tuple-element.1332, f32[512]{0:T(512)S(1)} %get-tuple-element.1331, f32[512]{0:T(512)S(1)} %get-tuple-element.1330, f32[512]{0:T(512)S(1)} %get-tuple-element.1329, f32[512]{0:T(512)S(1)} %get-tuple-element.1328, ...), kind=kLoop, calls=%fused_computation.24.clone.1 | loop fusion | flops 13107200 | bytes 1067008 | tf_op jit(solution)/shard_map/convert_element_type | solution.py:41
  52.3 7.9 %collective-permute-done.1 = bf16[1024,137]{1,0:T(8,128)(2,1)S(1)} collective-permute-done((bf16[1024,137]{1,0:T(8,128)(2,1)S(1)}, bf16[1024,137]{1,0:T(8,128)(2,1)S(1)}, u32[]{:S(2)}, u32[]{:S(2)}) %collective-permute-start.1) | collective-permute-done | bytes 280608 | tf_op jit(solution)/shard_map/while/body/eval_jaxpr/ppermute | solution.py:28
  60.2 1.6 while.121
  61.8 1.9 %add_convert_fusion.5 = bf16[512,1024]{1,0:T(8,128)(2,1)S(1)} fusion(f32[512]{0:T(512)S(1)} %get-tuple-element.1334, f32[512]{0:T(512)S(1)} %get-tuple-element.1332, f32[512]{0:T(512)S(1)} %get-tuple-element.1331, f32[512]{0:T(512)S(1)} %get-tuple-element.1330, f32[512]{0:T(512)S(1)} %get-tuple-element.1329, f32[512]{0:T(512)S(1)} %get-tuple-element.1328, ...), kind=kLoop, calls=%fused_computation.24.clone.1 | loop fusion | flops 13107200 | bytes 1067008 | tf_op jit(solution)/shard_map/convert_element_type | solution.py:41
  63.7 7.9 %collective-permute-done.1 = bf16[1024,137]{1,0:T(8,128)(2,1)S(1)} collective-permute-done((bf16[1024,137]{1,0:T(8,128)(2,1)S(1)}, bf16[1024,137]{1,0:T(8,128)(2,1)S(1)}, u32[]{:S(2)}, u32[]{:S(2)}) %collective-permute-start.1) | collective-permute-done | bytes 280608 | tf_op jit(solution)/shard_map/while/body/eval_jaxpr/ppermute | solution.py:28
  71.6 1.6 while.121
  73.3 1.9 %add_convert_fusion.5 = bf16[512,1024]{1,0:T(8,128)(2,1)S(1)} fusion(f32[512]{0:T(512)S(1)} %get-tuple-element.1334, f32[512]{0:T(512)S(1)} %get-tuple-element.1332, f32[512]{0:T(512)S(1)} %get-tuple-element.1331, f32[512]{0:T(512)S(1)} %get-tuple-element.1330, f32[512]{0:T(512)S(1)} %get-tuple-element.1329, f32[512]{0:T(512)S(1)} %get-tuple-element.1328, ...), kind=kLoop, calls=%fused_computation.24.clone.1 | loop fusion | flops 13107200 | bytes 1067008 | tf_op jit(solution)/shard_map/convert_element_type | solution.py:41
  75.2 7.9 %collective-permute-done.1 = bf16[1024,137]{1,0:T(8,128)(2,1)S(1)} collective-permute-done((bf16[1024,137]{1,0:T(8,128)(2,1)S(1)}, bf16[1024,137]{1,0:T(8,128)(2,1)S(1)}, u32[]{:S(2)}, u32[]{:S(2)}) %collective-permute-start.1) | collective-permute-done | bytes 280608 | tf_op jit(solution)/shard_map/while/body/eval_jaxpr/ppermute | solution.py:28
  84.8 1.9 %add_convert_fusion.5 = bf16[512,1024]{1,0:T(8,128)(2,1)S(1)} fusion(f32[512]{0:T(512)S(1)} %get-tuple-element.1334, f32[512]{0:T(512)S(1)} %get-tuple-element.1332, f32[512]{0:T(512)S(1)} %get-tuple-element.1331, f32[512]{0:T(512)S(1)} %get-tuple-element.1330, f32[512]{0:T(512)S(1)} %get-tuple-element.1329, f32[512]{0:T(512)S(1)} %get-tuple-element.1328, ...), kind=kLoop, calls=%fused_computation.24.clone.1 | loop fusion | flops 13107200 | bytes 1067008 | tf_op jit(solution)/shard_map/convert_element_type | solution.py:41
  86.7 7.9 %collective-permute-done.1 = bf16[1024,137]{1,0:T(8,128)(2,1)S(1)} collective-permute-done((bf16[1024,137]{1,0:T(8,128)(2,1)S(1)}, bf16[1024,137]{1,0:T(8,128)(2,1)S(1)}, u32[]{:S(2)}, u32[]{:S(2)}) %collective-permute-start.1) | collective-permute-done | bytes 280608 | tf_op jit(solution)/shard_map/while/body/eval_jaxpr/ppermute | solution.py:28
  97.3 5.6 %while.116 = (s32[]{:T(128)}, f32[1024,137]{0,1:T(8,128)S(1)}, s32[]{:T(128)}, bf16[512,1024]{1,0:T(8,128)(2,1)}, f32[512]{0:T(512)S(1)}, /*index=5*/bf16[512,13...) while((s32[]{:T(128)}, f32[1024,137]{0,1:T(8,128)S(1)}, s32[]{:T(128)}, ...), condition=%wide.region_7.8_spmd, body=%wide.region_6.7_spmd.sunk | while | flops 36106628 | bytes 1481367 | solution.py:73
  102.9 52.5 %while.120 = (s32[]{:T(128)}, f32[1024,137]{0,1:T(8,128)S(1)}, s32[]{:T(128)}, s32[512]{0:T(512)S(1)}, f32[512]{0:T(512)S(1)}, /*index=5*/s32[]{:T(128)}, bf16[5...) while((s32[]{:T(128)}, f32[1024,137]{0,1:T(8,128)S(1)}, ...), condition=%wide.region_11.12_spmd.clone, body=%wide.region_8.11_spmd.clone.sunk | while | flops 49638288 | bytes 6483061 | solution.py:125
  103.0 1.9 %add_convert_fusion.6 = bf16[512,1024]{1,0:T(8,128)(2,1)S(1)} fusion(f32[512]{0:T(512)S(1)} %get-tuple-element.1438, f32[512]{0:T(512)S(1)} %get-tuple-element.1436, f32[512]{0:T(512)S(1)} %get-tuple-element.1435, f32[512]{0:T(512)S(1)} %get-tuple-element.1434, f32[512]{0:T(512)S(1)} %get-tuple-element.1433, f32[512]{0:T(512)S(1)} %get-tuple-element.1432, ...), kind=kLoop, calls=%fused_computation.36.clone.1 | loop fusion | flops 13107200 | bytes 1067008 | tf_op jit(solution)/shard_map/convert_element_type | solution.py:41
  105.0 1.9 %while.122 = (s32[]{:T(128)}, f32[1024,137]{0,1:T(8,128)S(1)}, s32[]{:T(128)}, bf16[512,1024]{1,0:T(8,128)(2,1)S(1)}, f32[512]{0:T(512)S(1)}, /*index=5*/bf16[51...) while((s32[]{:T(128)}, f32[1024,137]{0,1:T(8,128)S(1)}, s32[]{:T(128)}, ...), condition=%wide.region_10.10_spmd, body=%wide.region_9.9_spmd.sunk | while | flops 36106628 | bytes 1481367 | solution.py:73
  106.9 3.5 %collective-permute-done = bf16[1024,137]{0,1:T(8,128)(2,1)S(1)} collective-permute-done((bf16[1024,137]{0,1:T(8,128)(2,1)S(1)}, bf16[1024,137]{0,1:T(8,128)(2,1)S(1)}, u32[]{:S(2)}, u32[]{:S(2)}) %collective-permute-start) | collective-permute-done | bytes 280608 | tf_op jit(solution)/shard_map/while/body/eval_jaxpr/ppermute | solution.py:28
  110.5 1.9 %add_convert_fusion.6 = bf16[512,1024]{1,0:T(8,128)(2,1)S(1)} fusion(f32[512]{0:T(512)S(1)} %get-tuple-element.1438, f32[512]{0:T(512)S(1)} %get-tuple-element.1436, f32[512]{0:T(512)S(1)} %get-tuple-element.1435, f32[512]{0:T(512)S(1)} %get-tuple-element.1434, f32[512]{0:T(512)S(1)} %get-tuple-element.1433, f32[512]{0:T(512)S(1)} %get-tuple-element.1432, ...), kind=kLoop, calls=%fused_computation.36.clone.1 | loop fusion | flops 13107200 | bytes 1067008 | tf_op jit(solution)/shard_map/convert_element_type | solution.py:41
  112.5 1.9 %while.122 = (s32[]{:T(128)}, f32[1024,137]{0,1:T(8,128)S(1)}, s32[]{:T(128)}, bf16[512,1024]{1,0:T(8,128)(2,1)S(1)}, f32[512]{0:T(512)S(1)}, /*index=5*/bf16[51...) while((s32[]{:T(128)}, f32[1024,137]{0,1:T(8,128)S(1)}, s32[]{:T(128)}, ...), condition=%wide.region_10.10_spmd, body=%wide.region_9.9_spmd.sunk | while | flops 36106628 | bytes 1481367 | solution.py:73
  114.4 3.5 %collective-permute-done = bf16[1024,137]{0,1:T(8,128)(2,1)S(1)} collective-permute-done((bf16[1024,137]{0,1:T(8,128)(2,1)S(1)}, bf16[1024,137]{0,1:T(8,128)(2,1)S(1)}, u32[]{:S(2)}, u32[]{:S(2)}) %collective-permute-start) | collective-permute-done | bytes 280608 | tf_op jit(solution)/shard_map/while/body/eval_jaxpr/ppermute | solution.py:28
  118.0 1.9 %add_convert_fusion.6 = bf16[512,1024]{1,0:T(8,128)(2,1)S(1)} fusion(f32[512]{0:T(512)S(1)} %get-tuple-element.1438, f32[512]{0:T(512)S(1)} %get-tuple-element.1436, f32[512]{0:T(512)S(1)} %get-tuple-element.1435, f32[512]{0:T(512)S(1)} %get-tuple-element.1434, f32[512]{0:T(512)S(1)} %get-tuple-element.1433, f32[512]{0:T(512)S(1)} %get-tuple-element.1432, ...), kind=kLoop, calls=%fused_computation.36.clone.1 | loop fusion | flops 13107200 | bytes 1067008 | tf_op jit(solution)/shard_map/convert_element_type | solution.py:41
  120.0 1.9 %while.122 = (s32[]{:T(128)}, f32[1024,137]{0,1:T(8,128)S(1)}, s32[]{:T(128)}, bf16[512,1024]{1,0:T(8,128)(2,1)S(1)}, f32[512]{0:T(512)S(1)}, /*index=5*/bf16[51...) while((s32[]{:T(128)}, f32[1024,137]{0,1:T(8,128)S(1)}, s32[]{:T(128)}, ...), condition=%wide.region_10.10_spmd, body=%wide.region_9.9_spmd.sunk | while | flops 36106628 | bytes 1481367 | solution.py:73
  121.9 3.5 %collective-permute-done = bf16[1024,137]{0,1:T(8,128)(2,1)S(1)} collective-permute-done((bf16[1024,137]{0,1:T(8,128)(2,1)S(1)}, bf16[1024,137]{0,1:T(8,128)(2,1)S(1)}, u32[]{:S(2)}, u32[]{:S(2)}) %collective-permute-start) | collective-permute-done | bytes 280608 | tf_op jit(solution)/shard_map/while/body/eval_jaxpr/ppermute | solution.py:28
  125.5 1.9 %add_convert_fusion.6 = bf16[512,1024]{1,0:T(8,128)(2,1)S(1)} fusion(f32[512]{0:T(512)S(1)} %get-tuple-element.1438, f32[512]{0:T(512)S(1)} %get-tuple-element.1436, f32[512]{0:T(512)S(1)} %get-tuple-element.1435, f32[512]{0:T(512)S(1)} %get-tuple-element.1434, f32[512]{0:T(512)S(1)} %get-tuple-element.1433, f32[512]{0:T(512)S(1)} %get-tuple-element.1432, ...), kind=kLoop, calls=%fused_computation.36.clone.1 | loop fusion | flops 13107200 | bytes 1067008 | tf_op jit(solution)/shard_map/convert_element_type | solution.py:41
  127.5 1.9 %while.122 = (s32[]{:T(128)}, f32[1024,137]{0,1:T(8,128)S(1)}, s32[]{:T(128)}, bf16[512,1024]{1,0:T(8,128)(2,1)S(1)}, f32[512]{0:T(512)S(1)}, /*index=5*/bf16[51...) while((s32[]{:T(128)}, f32[1024,137]{0,1:T(8,128)S(1)}, s32[]{:T(128)}, ...), condition=%wide.region_10.10_spmd, body=%wide.region_9.9_spmd.sunk | while | flops 36106628 | bytes 1481367 | solution.py:73
  129.4 3.5 %collective-permute-done = bf16[1024,137]{0,1:T(8,128)(2,1)S(1)} collective-permute-done((bf16[1024,137]{0,1:T(8,128)(2,1)S(1)}, bf16[1024,137]{0,1:T(8,128)(2,1)S(1)}, u32[]{:S(2)}, u32[]{:S(2)}) %collective-permute-start) | collective-permute-done | bytes 280608 | tf_op jit(solution)/shard_map/while/body/eval_jaxpr/ppermute | solution.py:28
  133.0 1.9 %add_convert_fusion.6 = bf16[512,1024]{1,0:T(8,128)(2,1)S(1)} fusion(f32[512]{0:T(512)S(1)} %get-tuple-element.1438, f32[512]{0:T(512)S(1)} %get-tuple-element.1436, f32[512]{0:T(512)S(1)} %get-tuple-element.1435, f32[512]{0:T(512)S(1)} %get-tuple-element.1434, f32[512]{0:T(512)S(1)} %get-tuple-element.1433, f32[512]{0:T(512)S(1)} %get-tuple-element.1432, ...), kind=kLoop, calls=%fused_computation.36.clone.1 | loop fusion | flops 13107200 | bytes 1067008 | tf_op jit(solution)/shard_map/convert_element_type | solution.py:41
  135.0 1.9 %while.122 = (s32[]{:T(128)}, f32[1024,137]{0,1:T(8,128)S(1)}, s32[]{:T(128)}, bf16[512,1024]{1,0:T(8,128)(2,1)S(1)}, f32[512]{0:T(512)S(1)}, /*index=5*/bf16[51...) while((s32[]{:T(128)}, f32[1024,137]{0,1:T(8,128)S(1)}, s32[]{:T(128)}, ...), condition=%wide.region_10.10_spmd, body=%wide.region_9.9_spmd.sunk | while | flops 36106628 | bytes 1481367 | solution.py:73
  136.9 3.5 %collective-permute-done = bf16[1024,137]{0,1:T(8,128)(2,1)S(1)} collective-permute-done((bf16[1024,137]{0,1:T(8,128)(2,1)S(1)}, bf16[1024,137]{0,1:T(8,128)(2,1)S(1)}, u32[]{:S(2)}, u32[]{:S(2)}) %collective-permute-start) | collective-permute-done | bytes 280608 | tf_op jit(solution)/shard_map/while/body/eval_jaxpr/ppermute | solution.py:28
  140.5 1.9 %add_convert_fusion.6 = bf16[512,1024]{1,0:T(8,128)(2,1)S(1)} fusion(f32[512]{0:T(512)S(1)} %get-tuple-element.1438, f32[512]{0:T(512)S(1)} %get-tuple-element.1436, f32[512]{0:T(512)S(1)} %get-tuple-element.1435, f32[512]{0:T(512)S(1)} %get-tuple-element.1434, f32[512]{0:T(512)S(1)} %get-tuple-element.1433, f32[512]{0:T(512)S(1)} %get-tuple-element.1432, ...), kind=kLoop, calls=%fused_computation.36.clone.1 | loop fusion | flops 13107200 | bytes 1067008 | tf_op jit(solution)/shard_map/convert_element_type | solution.py:41
  142.5 1.9 %while.122 = (s32[]{:T(128)}, f32[1024,137]{0,1:T(8,128)S(1)}, s32[]{:T(128)}, bf16[512,1024]{1,0:T(8,128)(2,1)S(1)}, f32[512]{0:T(512)S(1)}, /*index=5*/bf16[51...) while((s32[]{:T(128)}, f32[1024,137]{0,1:T(8,128)S(1)}, s32[]{:T(128)}, ...), condition=%wide.region_10.10_spmd, body=%wide.region_9.9_spmd.sunk | while | flops 36106628 | bytes 1481367 | solution.py:73
  144.4 3.5 %collective-permute-done = bf16[1024,137]{0,1:T(8,128)(2,1)S(1)} collective-permute-done((bf16[1024,137]{0,1:T(8,128)(2,1)S(1)}, bf16[1024,137]{0,1:T(8,128)(2,1)S(1)}, u32[]{:S(2)}, u32[]{:S(2)}) %collective-permute-start) | collective-permute-done | bytes 280608 | tf_op jit(solution)/shard_map/while/body/eval_jaxpr/ppermute | solution.py:28
  148.0 1.9 %add_convert_fusion.6 = bf16[512,1024]{1,0:T(8,128)(2,1)S(1)} fusion(f32[512]{0:T(512)S(1)} %get-tuple-element.1438, f32[512]{0:T(512)S(1)} %get-tuple-element.1436, f32[512]{0:T(512)S(1)} %get-tuple-element.1435, f32[512]{0:T(512)S(1)} %get-tuple-element.1434, f32[512]{0:T(512)S(1)} %get-tuple-element.1433, f32[512]{0:T(512)S(1)} %get-tuple-element.1432, ...), kind=kLoop, calls=%fused_computation.36.clone.1 | loop fusion | flops 13107200 | bytes 1067008 | tf_op jit(solution)/shard_map/convert_element_type | solution.py:41
  150.0 1.9 %while.122 = (s32[]{:T(128)}, f32[1024,137]{0,1:T(8,128)S(1)}, s32[]{:T(128)}, bf16[512,1024]{1,0:T(8,128)(2,1)S(1)}, f32[512]{0:T(512)S(1)}, /*index=5*/bf16[51...) while((s32[]{:T(128)}, f32[1024,137]{0,1:T(8,128)S(1)}, s32[]{:T(128)}, ...), condition=%wide.region_10.10_spmd, body=%wide.region_9.9_spmd.sunk | while | flops 36106628 | bytes 1481367 | solution.py:73
  151.9 3.5 %collective-permute-done = bf16[1024,137]{0,1:T(8,128)(2,1)S(1)} collective-permute-done((bf16[1024,137]{0,1:T(8,128)(2,1)S(1)}, bf16[1024,137]{0,1:T(8,128)(2,1)S(1)}, u32[]{:S(2)}, u32[]{:S(2)}) %collective-permute-start) | collective-permute-done | bytes 280608 | tf_op jit(solution)/shard_map/while/body/eval_jaxpr/ppermute | solution.py:28
  157.7 3.0 %collective-permute-done.4 = f32[256,137]{0,1:T(8,128)S(1)} collective-permute-done((f32[256,137]{0,1:T(8,128)S(1)}, f32[256,137]{0,1:T(8,128)S(1)}, u32[]{:S(2)}, u32[]{:S(2)}) %collective-permute-start.4) | collective-permute-done | bytes 140320 | tf_op jit(solution)/shard_map/ppermute | solution.py:28
  161.0 3.8 %collective-permute-done.5 = f32[256,137]{0,1:T(8,128)S(1)} collective-permute-done((f32[256,137]{0,1:T(8,128)S(1)}, f32[256,137]{0,1:T(8,128)S(1)}, u32[]{:S(2)}, u32[]{:S(2)}) %collective-permute-start.5) | collective-permute-done | bytes 140320 | tf_op jit(solution)/shard_map/ppermute | solution.py:28
  (227 shorter events, 43.6 us)
Async XLA Ops:
  0.6 95.6 %copy-start = (bf16[137,128]{1,0:T(8,128)(2,1)S(1)}, bf16[137,128]{1,0:T(8,128)(2,1)}, u32[]{:S(2)}) copy-start(bf16[137,128]{1,0:T(8,128)(2,1)} %param.32) | copy-start | bytes 105220
  0.6 6.0 %copy-start.7 = (s32[512]{0:T(512)S(1)}, s32[512]{0:T(512)}, u32[]{:S(2)}) copy-start(s32[512]{0:T(512)} %param.26) | copy-start | bytes 6148
  0.7 6.0 %copy-start.6 = (s32[512]{0:T(512)S(1)}, s32[512]{0:T(512)}, u32[]{:S(2)}) copy-start(s32[512]{0:T(512)} %param.28) | copy-start | bytes 6148
  0.7 6.0 %copy-start.5 = (f32[512]{0:T(512)S(1)}, f32[512]{0:T(512)}, u32[]{:S(2)}) copy-start(f32[512]{0:T(512)} %param.29) | copy-start | bytes 6148
  1.8 6.8 %collective-permute-start.2 = (bf16[256,137]{1,0:T(8,128)(2,1)S(1)}, bf16[256,137]{1,0:T(8,128)(2,1)S(1)}, u32[]{:S(2)}, u32[]{:S(2)}) collective-permute-start(bf16[256,137]{1,0:T(8,128)(2,1)S(1)} %get-tuple-element.793), channel_id=1, source_target_pairs={{0,1},{1,2},{2,3},{3,4},{4,5},{5,6},{6,7},{7,8},{8,9},{9,10},{10,1... | collective-permute-start | bytes 210440 | tf_op jit(solution)/shard_map/ppermute | solution.py:16
  4.9 8.3 %collective-permute-start.3 = (bf16[256,137]{1,0:T(8,128)(2,1)S(1)}, bf16[256,137]{1,0:T(8,128)(2,1)S(1)}, u32[]{:S(2)}, u32[]{:S(2)}) collective-permute-start(bf16[256,137]{1,0:T(8,128)(2,1)S(1)} %get-tuple-element.794), channel_id=1, source_target_pairs={{1,0},{2,1},{3,2},{4,3},{5,4},{6,5},{7,6},{8,7},{9,8},{10,9},{11,1... | collective-permute-start | bytes 210440 | tf_op jit(solution)/shard_map/ppermute | solution.py:18
  14.9 1.0 copy-start.1
  14.9 81.3 %copy-start.4 = (f32[512,128]{1,0:T(8,128)S(1)}, f32[512,128]{1,0:T(8,128)}, u32[]{:S(2)}) copy-start(f32[512,128]{1,0:T(8,128)} %param.31) | copy-start | bytes 786436
  14.9 81.6 %copy-start.8 = (f32[128]{0:T(128)S(1)}, f32[128]{0:T(128)}, u32[]{:S(2)}) copy-start(f32[128]{0:T(128)} %param.33) | copy-start | bytes 1540
  15.9 9.8 %collective-permute-start.1 = (bf16[1024,137]{1,0:T(8,128)(2,1)S(1)}, bf16[1024,137]{1,0:T(8,128)(2,1)S(1)}, u32[]{:S(2)}, u32[]{:S(2)}) collective-permute-start(bf16[1024,137]{1,0:T(8,128)(2,1)S(1)} %get-tuple-element.1296), channel_id=1, source_target_pairs={{224,0},{0,32},{32,64},{64,96},{96,128},{128,160},{160,192},{192,2... | collective-permute-start | bytes 841736 | tf_op jit(solution)/shard_map/while/body/eval_jaxpr/ppermute | solution.py:28
  27.4 9.8 %collective-permute-start.1 = (bf16[1024,137]{1,0:T(8,128)(2,1)S(1)}, bf16[1024,137]{1,0:T(8,128)(2,1)S(1)}, u32[]{:S(2)}, u32[]{:S(2)}) collective-permute-start(bf16[1024,137]{1,0:T(8,128)(2,1)S(1)} %get-tuple-element.1296), channel_id=1, source_target_pairs={{224,0},{0,32},{32,64},{64,96},{96,128},{128,160},{160,192},{192,2... | collective-permute-start | bytes 841736 | tf_op jit(solution)/shard_map/while/body/eval_jaxpr/ppermute | solution.py:28
  38.9 9.8 %collective-permute-start.1 = (bf16[1024,137]{1,0:T(8,128)(2,1)S(1)}, bf16[1024,137]{1,0:T(8,128)(2,1)S(1)}, u32[]{:S(2)}, u32[]{:S(2)}) collective-permute-start(bf16[1024,137]{1,0:T(8,128)(2,1)S(1)} %get-tuple-element.1296), channel_id=1, source_target_pairs={{224,0},{0,32},{32,64},{64,96},{96,128},{128,160},{160,192},{192,2... | collective-permute-start | bytes 841736 | tf_op jit(solution)/shard_map/while/body/eval_jaxpr/ppermute | solution.py:28
  50.3 9.8 %collective-permute-start.1 = (bf16[1024,137]{1,0:T(8,128)(2,1)S(1)}, bf16[1024,137]{1,0:T(8,128)(2,1)S(1)}, u32[]{:S(2)}, u32[]{:S(2)}) collective-permute-start(bf16[1024,137]{1,0:T(8,128)(2,1)S(1)} %get-tuple-element.1296), channel_id=1, source_target_pairs={{224,0},{0,32},{32,64},{64,96},{96,128},{128,160},{160,192},{192,2... | collective-permute-start | bytes 841736 | tf_op jit(solution)/shard_map/while/body/eval_jaxpr/ppermute | solution.py:28
  61.8 9.8 %collective-permute-start.1 = (bf16[1024,137]{1,0:T(8,128)(2,1)S(1)}, bf16[1024,137]{1,0:T(8,128)(2,1)S(1)}, u32[]{:S(2)}, u32[]{:S(2)}) collective-permute-start(bf16[1024,137]{1,0:T(8,128)(2,1)S(1)} %get-tuple-element.1296), channel_id=1, source_target_pairs={{224,0},{0,32},{32,64},{64,96},{96,128},{128,160},{160,192},{192,2... | collective-permute-start | bytes 841736 | tf_op jit(solution)/shard_map/while/body/eval_jaxpr/ppermute | solution.py:28
  73.3 9.8 %collective-permute-start.1 = (bf16[1024,137]{1,0:T(8,128)(2,1)S(1)}, bf16[1024,137]{1,0:T(8,128)(2,1)S(1)}, u32[]{:S(2)}, u32[]{:S(2)}) collective-permute-start(bf16[1024,137]{1,0:T(8,128)(2,1)S(1)} %get-tuple-element.1296), channel_id=1, source_target_pairs={{224,0},{0,32},{32,64},{64,96},{96,128},{128,160},{160,192},{192,2... | collective-permute-start | bytes 841736 | tf_op jit(solution)/shard_map/while/body/eval_jaxpr/ppermute | solution.py:28
  84.8 9.8 %collective-permute-start.1 = (bf16[1024,137]{1,0:T(8,128)(2,1)S(1)}, bf16[1024,137]{1,0:T(8,128)(2,1)S(1)}, u32[]{:S(2)}, u32[]{:S(2)}) collective-permute-start(bf16[1024,137]{1,0:T(8,128)(2,1)S(1)} %get-tuple-element.1296), channel_id=1, source_target_pairs={{224,0},{0,32},{32,64},{64,96},{96,128},{128,160},{160,192},{192,2... | collective-permute-start | bytes 841736 | tf_op jit(solution)/shard_map/while/body/eval_jaxpr/ppermute | solution.py:28
  96.6 0.7 copy-start.2
  103.0 7.4 %collective-permute-start = (bf16[1024,137]{0,1:T(8,128)(2,1)S(1)}, bf16[1024,137]{0,1:T(8,128)(2,1)S(1)}, u32[]{:S(2)}, u32[]{:S(2)}) collective-permute-start(bf16[1024,137]{0,1:T(8,128)(2,1)S(1)} %convert_element_type.96), channel_id=1, source_target_pairs={{224,0},{0,32},{32,64},{64,96},{96,128},{128,160},{160,192},{192,2... | collective-permute-start | bytes 841736 | tf_op jit(solution)/shard_map/while/body/eval_jaxpr/ppermute | solution.py:28
  110.5 7.4 %collective-permute-start = (bf16[1024,137]{0,1:T(8,128)(2,1)S(1)}, bf16[1024,137]{0,1:T(8,128)(2,1)S(1)}, u32[]{:S(2)}, u32[]{:S(2)}) collective-permute-start(bf16[1024,137]{0,1:T(8,128)(2,1)S(1)} %convert_element_type.96), channel_id=1, source_target_pairs={{224,0},{0,32},{32,64},{64,96},{96,128},{128,160},{160,192},{192,2... | collective-permute-start | bytes 841736 | tf_op jit(solution)/shard_map/while/body/eval_jaxpr/ppermute | solution.py:28
  118.0 7.4 %collective-permute-start = (bf16[1024,137]{0,1:T(8,128)(2,1)S(1)}, bf16[1024,137]{0,1:T(8,128)(2,1)S(1)}, u32[]{:S(2)}, u32[]{:S(2)}) collective-permute-start(bf16[1024,137]{0,1:T(8,128)(2,1)S(1)} %convert_element_type.96), channel_id=1, source_target_pairs={{224,0},{0,32},{32,64},{64,96},{96,128},{128,160},{160,192},{192,2... | collective-permute-start | bytes 841736 | tf_op jit(solution)/shard_map/while/body/eval_jaxpr/ppermute | solution.py:28
  125.5 7.4 %collective-permute-start = (bf16[1024,137]{0,1:T(8,128)(2,1)S(1)}, bf16[1024,137]{0,1:T(8,128)(2,1)S(1)}, u32[]{:S(2)}, u32[]{:S(2)}) collective-permute-start(bf16[1024,137]{0,1:T(8,128)(2,1)S(1)} %convert_element_type.96), channel_id=1, source_target_pairs={{224,0},{0,32},{32,64},{64,96},{96,128},{128,160},{160,192},{192,2... | collective-permute-start | bytes 841736 | tf_op jit(solution)/shard_map/while/body/eval_jaxpr/ppermute | solution.py:28
  133.0 7.4 %collective-permute-start = (bf16[1024,137]{0,1:T(8,128)(2,1)S(1)}, bf16[1024,137]{0,1:T(8,128)(2,1)S(1)}, u32[]{:S(2)}, u32[]{:S(2)}) collective-permute-start(bf16[1024,137]{0,1:T(8,128)(2,1)S(1)} %convert_element_type.96), channel_id=1, source_target_pairs={{224,0},{0,32},{32,64},{64,96},{96,128},{128,160},{160,192},{192,2... | collective-permute-start | bytes 841736 | tf_op jit(solution)/shard_map/while/body/eval_jaxpr/ppermute | solution.py:28
  140.5 7.4 %collective-permute-start = (bf16[1024,137]{0,1:T(8,128)(2,1)S(1)}, bf16[1024,137]{0,1:T(8,128)(2,1)S(1)}, u32[]{:S(2)}, u32[]{:S(2)}) collective-permute-start(bf16[1024,137]{0,1:T(8,128)(2,1)S(1)} %convert_element_type.96), channel_id=1, source_target_pairs={{224,0},{0,32},{32,64},{64,96},{96,128},{128,160},{160,192},{192,2... | collective-permute-start | bytes 841736 | tf_op jit(solution)/shard_map/while/body/eval_jaxpr/ppermute | solution.py:28
  148.0 7.4 %collective-permute-start = (bf16[1024,137]{0,1:T(8,128)(2,1)S(1)}, bf16[1024,137]{0,1:T(8,128)(2,1)S(1)}, u32[]{:S(2)}, u32[]{:S(2)}) collective-permute-start(bf16[1024,137]{0,1:T(8,128)(2,1)S(1)} %convert_element_type.96), channel_id=1, source_target_pairs={{224,0},{0,32},{32,64},{64,96},{96,128},{128,160},{160,192},{192,2... | collective-permute-start | bytes 841736 | tf_op jit(solution)/shard_map/while/body/eval_jaxpr/ppermute | solution.py:28
  155.5 5.2 %collective-permute-start.4 = (f32[256,137]{0,1:T(8,128)S(1)}, f32[256,137]{0,1:T(8,128)S(1)}, u32[]{:S(2)}, u32[]{:S(2)}) collective-permute-start(f32[256,137]{0,1:T(8,128)S(1)} %get-tuple-element.792), channel_id=1, source_target_pairs={{31,0},{0,1},{1,2},{2,3},{3,4},{4,5},{5,6},{6,7},{7,8},{8,9},{9,10... | collective-permute-start | bytes 420872 | tf_op jit(solution)/shard_map/ppermute | solution.py:28
  156.3 8.5 %collective-permute-start.5 = (f32[256,137]{0,1:T(8,128)S(1)}, f32[256,137]{0,1:T(8,128)S(1)}, u32[]{:S(2)}, u32[]{:S(2)}) collective-permute-start(f32[256,137]{0,1:T(8,128)S(1)} %get-tuple-element.791), channel_id=1, source_target_pairs={{1,0},{2,1},{3,2},{4,3},{5,4},{6,5},{7,6},{8,7},{9,8},{10,9},{11,1... | collective-permute-start | bytes 420872 | tf_op jit(solution)/shard_map/ppermute | solution.py:28
  165.0 0.7 copy-start.3
where the time goes:
time: 166 us
  waiting for transfers between devices  91.1 us (55%)
  other arithmetic  29.9 us (18%)
  matrix products  25.3 us (15%)
  local copies, waits for them, and re-layouts  9.27 us (6%)
  starting transfers between devices  5.54 us (3%)
  loops' own time  3.08 us (2%)
    ppermute x16, waiting for transfers between devices, shifted(): return lax.ppermute(block, axis, route)  86.5 us
    convert_element_type x15, other arithmetic, footprint_matrix(): return matrix.astype(jnp.bfloat16)  27.9 us
    dot_general x32, matrix products, spread_one_block(): lax.dot_general(rows, part, (((0,), (0,)), ((), ())), preferred_element_t...  15.4 us
    dot_general x32, matrix products, gather_one_block(): part = jnp.dot(rows, wide, preferred_element_type=jnp.float32)  9.37 us
    ppermute x1, waiting for transfers between devices, with_halo(): lax.ppermute(head, axis, [((i + 1) % count, i) for i in range(count)])  4.61 us
  transfers between devices with their start and end apart: 18, of which 17 were waited for; matrix products, arithmetic and copies ran while one was open for 25% of the time, Pallas kernels for 0%

commit v1 on v0

v1 whole, which is shorter than its diff:
```python
import functools

import jax
import jax.numpy as jnp
from jax import lax
from jax.experimental import pallas as pl
from jax.experimental.pallas import tpu as pltpu
from jax.sharding import PartitionSpec as P

MESH = pl.DeviceIdType.MESH
F32 = jnp.float32
BF16 = jnp.bfloat16

META, Z, RS, AG, BK = 0, 12, 18, 24, 30
COPIES = 36


def nt(a, b):
    return lax.dot_general(a, b, (((1,), (1,)), ((), ())), preferred_element_type=F32)


def kernel(
    n_space, total_cols,
    state_ref, start_ref, w_ref, slot_ref, frac_ref, count_ref, obs_ref, jac_ref, inv_ref,
    dep_ref, adj_ref,
    m_start, m_w, m_slot, m_frac, foot, zbuf, acc, abuf, pout, relay, rin, sbuf, wide, wout, win, rim, obs_t, dep_t, inv_t,
    send, recv,
):
    t = lax.axis_index("tm")
    s = lax.axis_index("space")
    mate = t + 1 - 2 * lax.rem(t, 2)
    y1 = lax.rem(t + 2, 8)
    y2 = lax.rem(t + 4, 8)
    y3 = lax.rem(t + 6, 8)
    left = lax.rem(s + n_space - 1, n_space)
    right = lax.rem(s + 1, n_space)
    chans = 128
    half = 256

    barrier = pltpu.get_barrier_semaphore()
    for peer in ((mate, s), (y1, s), (y2, s), (y3, s), (t, left), (mate, left), (t, right), (mate, right)):
        pl.semaphore_signal(barrier, inc=1, device_id=peer, device_id_type=MESH)

    def copy(index, src, dst, device):
        return pltpu.make_async_remote_copy(
            src_ref=src, dst_ref=dst, send_sem=send.at[index], recv_sem=recv.at[index],
            device_id=device, device_id_type=MESH,
        )

    z = lax.dot_general(jac_ref[...], state_ref[...], (((0,), (0,)), ((), ())), preferred_element_type=F32).astype(BF16)
    zbuf[1, 0] = z[:, :half]
    zbuf[2, 0] = z[:, half:]

    pl.semaphore_wait(barrier, 8)

    z_copies = [
        copy(Z + 2, zbuf.at[1, 0], zbuf.at[3, 0], (t, left)),
        copy(Z + 3, zbuf.at[2, 0], zbuf.at[0, 0], (t, right)),
        copy(Z + 4, zbuf.at[1, 0], zbuf.at[3, 1], (mate, left)),
        copy(Z + 5, zbuf.at[2, 0], zbuf.at[0, 1], (mate, right)),
        copy(Z + 0, zbuf.at[1, 0], zbuf.at[1, 1], (mate, s)),
        copy(Z + 1, zbuf.at[2, 0], zbuf.at[2, 1], (mate, s)),
    ]
    meta = []
    for hop, peer in ((2, y2), (1, y1), (3, y3)):
        at = 3 - hop
        for kind, (src, dst) in enumerate(((start_ref, m_start), (w_ref, m_w), (slot_ref, m_slot), (frac_ref, m_frac))):
            meta.append(copy(META + 4 * at + kind, src, dst.at[at], (peer, s)))
    for c in z_copies[:4] + meta + z_copies[4:]:
        c.start()

    obs_t[...] = jnp.transpose(obs_ref[...])
    inv_t[...] = jnp.transpose(jnp.broadcast_to(inv_ref[...], (chans, chans)))

    def weight_of(slot, frac, held):
        return jnp.where(slot == held, 1.0 - frac, 0.0) + jnp.where(slot + 1 == held, frac, 0.0)

    def build(group, start, w, slot, frac):
        own = weight_of(slot, frac, t)
        other = weight_of(slot, frac, mate)
        for h in range(2):
            lanes = slice(h * half, (h + 1) * half)
            abuf[2 * group + h, 0:1, :] = own[:, lanes]
            abuf[2 * group + h, 1:2, :] = other[:, lanes]
        local = jnp.bitwise_and(start - s * 512 + 256, total_cols - 1)
        row = lax.broadcasted_iota(jnp.int32, (8, 512), 0)
        ahead = jnp.bitwise_and(row - local, 7)
        weights = w.astype(F32)
        turned = jnp.zeros((8, 512), F32)
        for k in range(8):
            turned = turned + jnp.where(ahead == k, weights[k : k + 1, :], 0.0)
        block = lax.shift_right_arithmetic(local - row + 7, 3)

        def rows(index, carry):
            parts = [jnp.where(block == index * 8 + m, turned, 0.0) for m in range(8)]
            value = jnp.concatenate(parts, axis=0).astype(BF16)
            at = pl.ds(pl.multiple_of(index * 64, 64), 64)
            foot[2 * group, at, :] = value[:, :half]
            foot[2 * group + 1, at, :] = value[:, half:]
            return carry

        lax.fori_loop(0, 16, rows, 0)

    build(0, start_ref[...], w_ref[...], slot_ref[...], frac_ref[...])

    def wait_meta(at):
        for kind, (src, dst) in enumerate(((start_ref, m_start), (w_ref, m_w), (slot_ref, m_slot), (frac_ref, m_frac))):
            copy(META + 4 * at + kind, src, dst.at[at], (y1, s)).wait_recv()

    for group in (2, 1, 3):
        at = group - 1
        wait_meta(at)
        build(group, m_start[at], m_w[at], m_slot[at], m_frac[at])

    z_copies[4].wait_recv()
    z_copies[5].wait_recv()

    def stacked(chunk):
        return jnp.concatenate([zbuf[chunk, 0], zbuf[chunk, 1]], axis=0)

    def centre(piece, carry):
        acc[piece] = jnp.dot(stacked(1), foot[piece, half : 2 * half], preferred_element_type=F32) + jnp.dot(
            stacked(2), foot[piece, 2 * half : 3 * half], preferred_element_type=F32
        )
        return carry

    lax.fori_loop(0, 8, centre, 0)

    for c in z_copies[:4]:
        c.wait_recv()

    def finish(piece):
        total = (
            acc[piece]
            + jnp.dot(stacked(0), foot[piece, 0:half], preferred_element_type=F32)
            + jnp.dot(stacked(3), foot[piece, 3 * half : 4 * half], preferred_element_type=F32)
        )
        return abuf[piece, 0:1, :] * total[:chans] + abuf[piece, 1:2, :] * total[chans:]

    pout[0] = finish(4).astype(BF16)
    pout[1] = finish(5).astype(BF16)
    rs = [
        copy(RS + 0, pout.at[0], relay.at[0], (y1, s)),
        copy(RS + 1, pout.at[1], relay.at[1], (y3, s)),
        copy(RS + 2, pout.at[2], rin.at[1], (y1, s)),
        copy(RS + 3, pout.at[3], rin.at[2], (y3, s)),
        copy(RS + 4, pout.at[4], rin.at[0], (y1, s)),
        copy(RS + 5, pout.at[5], rin.at[3], (y3, s)),
    ]
    rs[0].start()
    rs[1].start()
    pout[2] = finish(3).astype(BF16)
    rs[2].start()
    pout[3] = finish(6).astype(BF16)
    rs[3].start()
    first = finish(2)
    second = finish(7)
    rs[0].wait_recv()
    pout[4] = (first + relay[0].astype(F32)).astype(BF16)
    rs[4].start()
    rs[1].wait_recv()
    pout[5] = (second + relay[1].astype(F32)).astype(BF16)
    rs[5].start()
    acc[0, 0:chans] = finish(0)
    acc[1, 0:chans] = finish(1)

    count = count_ref[0, 0]
    column = lax.broadcasted_iota(jnp.int32, (1, half), 1)
    for h, waits in ((0, (rs[4], rs[3])), (1, (rs[2], rs[5]))):
        for c in waits:
            c.wait_recv()
        projected = acc[h, 0:chans] + rin[h].astype(F32) + rin[2 + h].astype(F32)
        live = column + h * half < count
        departed = jnp.where(live, obs_t[:, h * half : (h + 1) * half] - projected, 0.0)
        dep_t[:, h * half : (h + 1) * half] = departed
        sbuf[h] = (departed * inv_t[:, 0:1]).astype(BF16)

    ag = [
        copy(AG + 0, sbuf.at[0], sbuf.at[6], (y1, s)),
        copy(AG + 1, sbuf.at[1], sbuf.at[3], (y3, s)),
        copy(AG + 2, sbuf.at[1], sbuf.at[7], (y1, s)),
        copy(AG + 3, sbuf.at[0], sbuf.at[2], (y3, s)),
        copy(AG + 4, sbuf.at[6], sbuf.at[4], (y1, s)),
        copy(AG + 5, sbuf.at[3], sbuf.at[5], (y3, s)),
    ]
    for c in ag[:4]:
        c.start()
    dep_ref[...] = jnp.transpose(dep_t[...])

    def scaled_by_slot(piece):
        values = sbuf[piece].astype(F32)
        return jnp.concatenate(
            [(abuf[piece, 0:1, :] * values).astype(BF16), (abuf[piece, 1:2, :] * values).astype(BF16)], axis=0
        )

    def spread(piece, fresh):
        v = scaled_by_slot(piece)
        for chunk in (0, 3, 1, 2):
            part = nt(v, foot[piece, chunk * half : (chunk + 1) * half])
            if fresh:
                wide[chunk] = part
            else:
                wide[chunk] += part

    spread(0, True)
    spread(1, False)
    ag[0].wait_recv()
    ag[4].start()
    ag[1].wait_recv()
    ag[5].start()
    spread(6, False)
    spread(3, False)
    ag[2].wait_recv()
    spread(7, False)
    ag[3].wait_recv()
    spread(2, False)
    ag[4].wait_recv()
    spread(4, False)
    ag[5].wait_recv()
    spread(5, False)

    for place, chunk in enumerate((0, 3, 1, 2)):
        wout[place, 0] = wide[chunk, 0:chans].astype(BF16)
        wout[place, 1] = wide[chunk, chans:].astype(BF16)
    bk = [
        copy(BK + 0, wout.at[0, 0], rim.at[2], (t, left)),
        copy(BK + 1, wout.at[1, 0], rim.at[0], (t, right)),
        copy(BK + 2, wout.at[0, 1], rim.at[3], (mate, left)),
        copy(BK + 3, wout.at[1, 1], rim.at[1], (mate, right)),
        copy(BK + 4, wout.at[2, 1], win.at[0], (mate, s)),
        copy(BK + 5, wout.at[3, 1], win.at[1], (mate, s)),
    ]
    for c in bk:
        c.start()
    for h, waits in ((0, (bk[4], bk[1], bk[3])), (1, (bk[5], bk[0], bk[2]))):
        for c in waits:
            c.wait_recv()
        whole = wide[1 + h, 0:chans] + win[h].astype(F32) + rim[2 * h].astype(F32) + rim[2 * h + 1].astype(F32)
        adj_ref[:, h * half : (h + 1) * half] = jnp.dot(jac_ref[...], whole.astype(BF16), preferred_element_type=F32)

    for c in z_copies + meta + rs + ag + bk:
        c.wait_send()


def body(state, obs_start, foot_weight, obs_slot, obs_frac, live_count, obs_values, jacobian, inv_var):
    n_space = lax.axis_size("space")
    levels = jacobian.shape[0]
    vmem = pl.BlockSpec(memory_space=pltpu.VMEM)
    departures, adjoint = pl.pallas_call(
        functools.partial(kernel, n_space, 512 * n_space),
        out_shape=(
            jax.ShapeDtypeStruct((512, 128), F32),
            jax.ShapeDtypeStruct((levels, 512), F32),
        ),
        in_specs=[vmem] * 5 + [pl.BlockSpec(memory_space=pltpu.SMEM)] + [vmem] * 3,
        out_specs=(vmem, vmem),
        scratch_shapes=[
            pltpu.VMEM((3, 1, 512), jnp.int32),
            pltpu.VMEM((3, 8, 512), BF16),
            pltpu.VMEM((3, 1, 512), jnp.int32),
            pltpu.VMEM((3, 1, 512), F32),
            pltpu.VMEM((8, 1024, 256), BF16),
            pltpu.VMEM((4, 2, 128, 256), BF16),
            pltpu.VMEM((8, 256, 256), F32),
            pltpu.VMEM((8, 2, 256), F32),
            pltpu.VMEM((6, 128, 256), BF16),
            pltpu.VMEM((2, 128, 256), BF16),
            pltpu.VMEM((4, 128, 256), BF16),
            pltpu.VMEM((8, 128, 256), BF16),
            pltpu.VMEM((4, 256, 256), F32),
            pltpu.VMEM((4, 2, 128, 256), BF16),
            pltpu.VMEM((2, 128, 256), BF16),
            pltpu.VMEM((4, 128, 256), BF16),
            pltpu.VMEM((128, 512), F32),
            pltpu.VMEM((128, 512), F32),
            pltpu.VMEM((128, 128), F32),
            pltpu.SemaphoreType.DMA((COPIES,)),
            pltpu.SemaphoreType.DMA((COPIES,)),
        ],
        compiler_params=pltpu.CompilerParams(collective_id=0, has_side_effects=True),
        name="window",
    )(
        jnp.transpose(state[0]),
        obs_start[None],
        jnp.transpose(foot_weight),
        obs_slot[None],
        obs_frac[None],
        live_count,
        obs_values,
        jacobian,
        inv_var[None],
    )
    return departures, jnp.transpose(adjoint)[None]


def solution(mesh):
    return jax.shard_map(
        body,
        mesh=mesh,
        in_specs=(
            P("tm", "space", None),
            P(("tm", "space")),
            P(("tm", "space"), None),
            P(("tm", "space")),
            P(("tm", "space")),
            P("tm", "space"),
            P(("tm", "space"), None),
            P(),
            P(),
        ),
        out_specs=(P(("tm", "space"), None), P("tm", "space", None)),
        check_vma=False,
    )
```

time: 166 us -> 44.1 us (0.27)
  the two profiles are of different devices: /device:TPU:102 before, /device:TPU:1 now
where the time goes in v1:
time: 44.1 us; the launch traced here: 43.8 us
  Pallas kernels  39.8 us (90%)
  local copies, waits for them, and re-layouts  2.71 us (6%)
  between operations  1.29 us (3%)
    pallas_call x1, Pallas kernels, body(): pl.pallas_call(functools.partial(kernel, n_space, 512 * n_space), out_sha...  39.8 us
    unnamed x4, local copies, waits for them, and re-layouts  2.71 us

profile of v1, /device:TPU:1, one launch (start us, length us, event | category | flops | bytes accessed | tf_op | source)
XLA Modules:
  0.0 43.8 jit_solution(15048165388172368572)
XLA Ops:
  1.3 39.8 %window.1 = (f32[512,128]{1,0:T(8,128)}, f32[137,512]{1,0:T(8,128)}) custom-call(bf16[137,512]{1,0:T(8,128)(2,1)} %bitcast.12, s32[1,512]{1,0:T(1,128)} %bitcast.14, bf16[8,512]{1,0:T(8,128)(2,1)} %bitcast.13, s32[1,512]{1,0:T(1,128)} %bitcast.15, f32[1,512]{1,0:T(1,128)} %bitcast.16, s32[1,1]{1,0:T(1,128)S(6)} %copy.13.count_ref, f32[512,128]{1,0:T(8,128)} %obs_ref.1, ...), custom_call_target="tpu_custom_call" | custom-call | tf_op jit(solution)/shard_map/window/pallas_call | solution.py:249
  41.1 0.0 copy-start
  41.1 2.0 %copy.11 = f32[1,512,137]{1,0,2:T(1,128)} copy(f32[1,512,137]{1,2,0:T(8,128)} %bitcast.11) | data formatting | bytes 561152
  43.1 0.0 copy-done
  43.1 0.7 %copy.14 = f32[512,128]{1,0:T(8,128)} copy(f32[512,128]{1,0:T(8,128)S(1)} %copy-done) | data formatting | bytes 524288
Async XLA Ops:
  41.1 2.0 %copy-start = (f32[512,128]{1,0:T(8,128)S(1)}, f32[512,128]{1,0:T(8,128)}, u32[]{:S(2)}) copy-start(f32[512,128]{1,0:T(8,128)} %get-tuple-element.10) | copy-start | bytes 786436

commit v2 on v1

v2 whole, which is shorter than its diff:
```python
import functools

import jax
import jax.numpy as jnp
from jax import lax
from jax.experimental import pallas as pl
from jax.experimental.pallas import tpu as pltpu
from jax.sharding import PartitionSpec as P

MESH = pl.DeviceIdType.MESH
F32 = jnp.float32
BF16 = jnp.bfloat16

META, Z, RS, AG, BK = 0, 12, 18, 30, 42
COPIES = 48

LEFT, RIGHT, HEAD, TAIL = 0, 1, 2, 3


def nt(a, b):
    return lax.dot_general(a, b, (((1,), (1,)), ((), ())), preferred_element_type=F32)


def kernel(
    n_space, total_cols,
    state_in, start_in, w_in, slot_in, frac_in, count_ref, obs_in, jac_in, inv_in,
    dep_out, adj_out,
    state_ref, start_ref, w_ref, slot_ref, frac_ref, obs_ref, jac_ref, inv_ref, dep_ref, adj_ref,
    m_start, m_w, m_slot, m_frac, foot, zbuf, acc, abuf, pout, relay, rin, sbuf, wide, wout, win, rim, obs_t, inv_t, dep_t,
    load, store, send, recv,
):
    t = lax.axis_index("tm")
    s = lax.axis_index("space")
    mate = t + 1 - 2 * lax.rem(t, 2)
    y1 = lax.rem(t + 2, 8)
    y2 = lax.rem(t + 4, 8)
    y3 = lax.rem(t + 6, 8)
    left = lax.rem(s + n_space - 1, n_space)
    right = lax.rem(s + 1, n_space)
    chans = 128
    quarter = 128

    barrier = pltpu.get_barrier_semaphore()
    for peer in ((t, right), (t, left), (mate, left), (mate, right), (y2, s), (y1, s), (y3, s), (mate, s)):
        pl.semaphore_signal(barrier, inc=1, device_id=peer, device_id_type=MESH)

    loads = [
        pltpu.make_async_copy(src, dst, load.at[k])
        for k, (src, dst) in enumerate(
            (
                (state_in, state_ref), (jac_in, jac_ref), (start_in, start_ref), (w_in, w_ref), (slot_in, slot_ref),
                (frac_in, frac_ref), (obs_in, obs_ref), (inv_in, inv_ref),
            )
        )
    ]
    for c in loads:
        c.start()

    def copy(index, src, dst, device):
        return pltpu.make_async_remote_copy(
            src_ref=src, dst_ref=dst, send_sem=send.at[index], recv_sem=recv.at[index],
            device_id=device, device_id_type=MESH,
        )

    loads[0].wait()
    loads[1].wait()
    z = lax.dot_general(jac_ref[...], state_ref[...], (((0,), (0,)), ((), ())), preferred_element_type=F32).astype(BF16)
    zbuf[HEAD, 0] = z[:, :256]
    zbuf[TAIL, 0] = z[:, 256:]
    for c in loads[2:6]:
        c.wait()

    pl.semaphore_wait(barrier, 8)

    z_copies = [
        copy(Z + 0, zbuf.at[HEAD, 0], zbuf.at[RIGHT, 0], (t, left)),
        copy(Z + 1, zbuf.at[TAIL, 0], zbuf.at[LEFT, 0], (t, right)),
        copy(Z + 2, zbuf.at[HEAD, 0], zbuf.at[RIGHT, 1], (mate, left)),
        copy(Z + 3, zbuf.at[TAIL, 0], zbuf.at[LEFT, 1], (mate, right)),
        copy(Z + 4, zbuf.at[HEAD, 0], zbuf.at[HEAD, 1], (mate, s)),
        copy(Z + 5, zbuf.at[TAIL, 0], zbuf.at[TAIL, 1], (mate, s)),
    ]
    fields = ((start_ref, m_start), (w_ref, m_w), (slot_ref, m_slot), (frac_ref, m_frac))
    meta = {}
    for hop, peer in ((2, y2), (1, y1), (3, y3)):
        at = 3 - hop
        meta[at] = [copy(META + 4 * at + kind, src, dst.at[at], (peer, s)) for kind, (src, dst) in enumerate(fields)]
    for c in z_copies[:4] + meta[1] + meta[2] + meta[0] + z_copies[4:]:
        c.start()

    def weight_of(slot, frac, held):
        return jnp.where(slot == held, 1.0 - frac, 0.0) + jnp.where(slot + 1 == held, frac, 0.0)

    def build(group, start, w, slot, frac):
        abuf[group, 0:1, :] = weight_of(slot, frac, t)
        abuf[group, 1:2, :] = weight_of(slot, frac, mate)
        local = jnp.bitwise_and(start - s * 512 + 256, total_cols - 1)
        row = lax.broadcasted_iota(jnp.int32, (8, 512), 0)
        ahead = jnp.bitwise_and(row - local, 7)
        weights = w.astype(F32)
        turned = jnp.zeros((8, 512), F32)
        for k in range(8):
            turned = turned + jnp.where(ahead == k, weights[k : k + 1, :], 0.0)
        block = lax.shift_right_arithmetic(local - row + 7, 3)

        for first, last, shift in ((0, 4, 0), (4, 8, 8), (8, 16, -4)):

            def rows(index, carry):
                parts = [jnp.where(block == (index + shift) * 8 + m, turned, 0.0) for m in range(8)]
                at = pl.ds(pl.multiple_of(index * 64, 64), 64)
                foot[group, at, :] = jnp.concatenate(parts, axis=0).astype(BF16)
                return carry

            lax.fori_loop(first, last, rows, 0)

    def columns(first):
        return jnp.concatenate(
            [
                jnp.concatenate([zbuf[first, 0], zbuf[first + 1, 0]], axis=1),
                jnp.concatenate([zbuf[first, 1], zbuf[first + 1, 1]], axis=1),
            ],
            axis=0,
        )

    def centre(group):
        acc[group] = jnp.dot(columns(HEAD), foot[group, 512:1024, :], preferred_element_type=F32)

    build(0, start_ref[...], w_ref[...], slot_ref[...], frac_ref[...])
    for c in loads[6:]:
        c.wait()
    obs_t[...] = jnp.transpose(obs_ref[...])
    inv_t[...] = jnp.transpose(jnp.broadcast_to(inv_ref[...], (chans, chans)))
    z_copies[4].wait_recv()
    z_copies[5].wait_recv()
    centre(0)
    for group in (2, 1, 3):
        at = group - 1
        for c in meta[at]:
            c.wait_recv()
        build(group, m_start[at], m_w[at], m_slot[at], m_frac[at])
        centre(group)
    for c in z_copies[:4]:
        c.wait_recv()

    def finish(group):
        total = acc[group] + jnp.dot(columns(LEFT), foot[group, 0:512, :], preferred_element_type=F32)
        return abuf[group, 0:1, :] * total[:chans] + abuf[group, 1:2, :] * total[chans:]

    def lanes(q):
        return slice(q * quarter, (q + 1) * quarter)

    far = [copy(RS + q, pout.at[q], relay.at[q], ((y1, y1, y3, y3)[q], s)) for q in range(4)]
    to_next = [copy(RS + 4 + q, pout.at[4 + q], rin.at[0, q], (y1, s)) for q in range(4)]
    to_last = [copy(RS + 8 + q, pout.at[8 + q], rin.at[1, q], (y3, s)) for q in range(4)]
    partial = finish(2)
    for q in range(4):
        pout[q] = partial[:, lanes(q)].astype(BF16)
    for q in (0, 2, 1, 3):
        far[q].start()
    partial = finish(1)
    for q in (2, 3):
        pout[4 + q] = partial[:, lanes(q)].astype(BF16)
        to_next[q].start()
    acc[1, 0:chans, 0:256] = partial[:, :256]
    partial = finish(3)
    for q in (0, 1):
        pout[8 + q] = partial[:, lanes(q)].astype(BF16)
        to_last[q].start()
    acc[3, 0:chans, 256:512] = partial[:, 256:]
    acc[0, 0:chans] = finish(0)
    for q, group, base, copies in ((0, 1, 4, to_next), (2, 3, 8, to_last), (1, 1, 4, to_next), (3, 3, 8, to_last)):
        far[q].wait_recv()
        pout[base + q] = (acc[group, 0:chans, lanes(q)] + relay[q].astype(F32)).astype(BF16)
        copies[q].start()

    ag_next = [copy(AG + q, sbuf.at[0, q], sbuf.at[3, q], (y1, s)) for q in range(4)]
    ag_last = [copy(AG + 4 + q, sbuf.at[0, q], sbuf.at[1, q], (y3, s)) for q in range(4)]
    ag_far = [
        copy(AG + 8 + q, sbuf.at[(3, 3, 1, 1)[q], q], sbuf.at[2, q], ((y1, y1, y3, y3)[q], s)) for q in range(4)
    ]
    column = lax.broadcasted_iota(jnp.int32, (1, quarter), 1)
    for q in (0, 2, 1, 3):
        to_next[q].wait_recv()
        to_last[q].wait_recv()
        projected = acc[0, 0:chans, lanes(q)] + rin[0, q].astype(F32) + rin[1, q].astype(F32)
        live = column + q * quarter < count_ref[0, 0]
        departed = jnp.where(live, obs_t[:, lanes(q)] - projected, 0.0)
        dep_t[:, lanes(q)] = departed
        sbuf[0, q] = (departed * inv_t[:, 0:1]).astype(BF16)
        (ag_next if q < 2 else ag_last)[q].start()
    ag_next[2].start()
    ag_last[0].start()
    ag_next[3].start()
    ag_last[1].start()

    dep_ref[...] = jnp.transpose(dep_t[...])
    stores = [
        pltpu.make_async_copy(dep_ref, dep_out, store.at[0]),
        pltpu.make_async_copy(adj_ref.at[:, :, 0:256], adj_out.at[:, :, 0:256], store.at[1]),
        pltpu.make_async_copy(adj_ref.at[:, :, 256:512], adj_out.at[:, :, 256:512], store.at[2]),
    ]
    stores[0].start()

    def by_slot(group, quarters):
        values = jnp.concatenate([sbuf[group, q] for q in quarters], axis=1).astype(F32)
        span = slice(quarters[0] * quarter, (quarters[-1] + 1) * quarter)
        return jnp.concatenate(
            [(abuf[group, 0:1, span] * values).astype(BF16), (abuf[group, 1:2, span] * values).astype(BF16)], axis=0
        )

    def spread(group, quarters, fresh=False):
        v = by_slot(group, quarters)
        span = slice(quarters[0] * quarter, (quarters[-1] + 1) * quarter)
        for chunk in range(4):
            part = nt(v, foot[group, chunk * 256 : (chunk + 1) * 256, span])
            if fresh:
                wide[chunk] = part
            else:
                wide[chunk] += part

    spread(0, (0, 1, 2, 3), True)
    for q in (0, 2, 1, 3):
        (ag_next if q < 2 else ag_last)[q].wait_recv()
        ag_far[q].start()
    spread(3, (0, 1))
    spread(1, (2, 3))
    ag_next[2].wait_recv()
    ag_next[3].wait_recv()
    spread(3, (2, 3))
    ag_last[0].wait_recv()
    ag_last[1].wait_recv()
    spread(1, (0, 1))
    for q in (0, 2, 1, 3):
        ag_far[q].wait_recv()
    bk = [
        copy(BK + 0, wout.at[LEFT, 0], rim.at[1, 0], (t, left)),
        copy(BK + 1, wout.at[RIGHT, 0], rim.at[0, 0], (t, right)),
        copy(BK + 2, wout.at[LEFT, 1], rim.at[1, 1], (mate, left)),
        copy(BK + 3, wout.at[RIGHT, 1], rim.at[0, 1], (mate, right)),
        copy(BK + 4, wout.at[HEAD, 1], win.at[0], (mate, s)),
        copy(BK + 5, wout.at[TAIL, 1], win.at[1], (mate, s)),
    ]
    v = by_slot(2, (0, 1, 2, 3))
    for chunk in (LEFT, RIGHT):
        total = wide[chunk] + nt(v, foot[2, chunk * 256 : (chunk + 1) * 256, :])
        wout[chunk, 0] = total[:chans].astype(BF16)
        wout[chunk, 1] = total[chans:].astype(BF16)
        bk[chunk].start()
        bk[2 + chunk].start()
    for chunk in (HEAD, TAIL):
        total = wide[chunk] + nt(v, foot[2, chunk * 256 : (chunk + 1) * 256, :])
        wide[chunk] = total
        wout[chunk, 1] = total[chans:].astype(BF16)
        bk[2 + chunk].start()
    for h, waits in ((0, (bk[4], bk[1], bk[3])), (1, (bk[5], bk[0], bk[2]))):
        for c in waits:
            c.wait_recv()
        whole = wide[HEAD + h, 0:chans] + win[h].astype(F32) + rim[h, 0].astype(F32) + rim[h, 1].astype(F32)
        adj_ref[:, 0, h * 256 : (h + 1) * 256] = jnp.dot(jac_ref[...], whole.astype(BF16), preferred_element_type=F32)
        stores[1 + h].start()
    for c in z_copies + meta[0] + meta[1] + meta[2] + far + to_next + to_last + ag_next + ag_last + ag_far + bk:
        c.wait_send()
    for c in stores:
        c.wait()


def body(state, obs_start, foot_weight, obs_slot, obs_frac, live_count, obs_values, jacobian, inv_var):
    n_space = lax.axis_size("space")
    levels = jacobian.shape[0]
    anywhere = pl.BlockSpec(memory_space=pl.ANY)
    i32 = jnp.int32
    departures, adjoint = pl.pallas_call(
        functools.partial(kernel, n_space, 512 * n_space),
        out_shape=(
            jax.ShapeDtypeStruct((512, 128), F32),
            jax.ShapeDtypeStruct((levels, 1, 512), F32),
        ),
        in_specs=[anywhere] * 5 + [pl.BlockSpec(memory_space=pltpu.SMEM)] + [anywhere] * 3,
        out_specs=(anywhere, anywhere),
        scratch_shapes=[
            pltpu.VMEM((levels, 512), BF16),
            pltpu.VMEM((1, 512), i32),
            pltpu.VMEM((8, 512), BF16),
            pltpu.VMEM((1, 512), i32),
            pltpu.VMEM((1, 512), F32),
            pltpu.VMEM((512, 128), F32),
            pltpu.VMEM((levels, 128), BF16),
            pltpu.VMEM((1, 128), F32),
            pltpu.VMEM((512, 128), F32),
            pltpu.VMEM((levels, 1, 512), F32),
            pltpu.VMEM((3, 1, 512), i32),
            pltpu.VMEM((3, 8, 512), BF16),
            pltpu.VMEM((3, 1, 512), i32),
            pltpu.VMEM((3, 1, 512), F32),
            pltpu.VMEM((4, 1024, 512), BF16),
            pltpu.VMEM((4, 2, 128, 256), BF16),
            pltpu.VMEM((4, 256, 512), F32),
            pltpu.VMEM((4, 2, 512), F32),
            pltpu.VMEM((12, 128, 128), BF16),
            pltpu.VMEM((4, 128, 128), BF16),
            pltpu.VMEM((2, 4, 128, 128), BF16),
            pltpu.VMEM((4, 4, 128, 128), BF16),
            pltpu.VMEM((4, 256, 256), F32),
            pltpu.VMEM((4, 2, 128, 256), BF16),
            pltpu.VMEM((2, 128, 256), BF16),
            pltpu.VMEM((2, 2, 128, 256), BF16),
            pltpu.VMEM((128, 512), F32),
            pltpu.VMEM((128, 128), F32),
            pltpu.VMEM((128, 512), F32),
            pltpu.SemaphoreType.DMA((8,)),
            pltpu.SemaphoreType.DMA((3,)),
            pltpu.SemaphoreType.DMA((COPIES,)),
            pltpu.SemaphoreType.DMA((COPIES,)),
        ],
        compiler_params=pltpu.CompilerParams(collective_id=0, has_side_effects=True),
        name="window",
    )(
        jnp.transpose(state[0]),
        obs_start[None],
        jnp.transpose(foot_weight),
        obs_slot[None],
        obs_frac[None],
        live_count,
        obs_values,
        jacobian,
        inv_var[None],
    )
    return departures, jnp.transpose(adjoint, (1, 2, 0))


def solution(mesh):
    return jax.shard_map(
        body,
        mesh=mesh,
        in_specs=(
            P("tm", "space", None),
            P(("tm", "space")),
            P(("tm", "space"), None),
            P(("tm", "space")),
            P(("tm", "space")),
            P("tm", "space"),
            P(("tm", "space"), None),
            P(),
            P(),
        ),
        out_specs=(P(("tm", "space"), None), P("tm", "space", None)),
        check_vma=False,
    )
```

time: 44.1 us -> 43 us (0.975)
  Pallas kernels: 39.8 us -> 39.2 us
    pallas_call x1, Pallas kernels: 39.8 us -> 39.2 us  [body(): pl.pallas_call(functools.partial(kernel, n_space, 512 * n_space), out_sha...]
where the time goes in v2:
time: 43 us; the launch traced here: 42.9 us
  Pallas kernels  39.2 us (91%)
  local copies, waits for them, and re-layouts  2.43 us (6%)
  between operations  1.29 us (3%)
    pallas_call x1, Pallas kernels, body(): pl.pallas_call(functools.partial(kernel, n_space, 512 * n_space), out_sha...  39.2 us
    unnamed x4, local copies, waits for them, and re-layouts  2.43 us

profile of v2, /device:TPU:1, one launch (start us, length us, event | category | flops | bytes accessed | tf_op | source)
XLA Modules:
  0.0 42.9 jit_solution(3785178679287093059)
XLA Ops:
  1.3 39.2 %window.1 = (f32[512,128]{1,0:T(8,128)}, f32[137,1,512]{2,1,0:T(1,128)}) custom-call(bf16[137,512]{1,0:T(8,128)(2,1)} %bitcast.10, s32[1,512]{1,0:T(1,128)} %bitcast.12, bf16[8,512]{1,0:T(8,128)(2,1)} %bitcast.11, s32[1,512]{1,0:T(1,128)} %bitcast.13, f32[1,512]{1,0:T(1,128)} %bitcast.14, s32[1,1]{1,0:T(1,128)S(6)} %copy.13.count_ref, f32[512,128]{1,0:T(8,128)} %obs_in.1, ...), custom_call_target="tpu_custom_call" | custom-call | tf_op jit(solution)/shard_map/window/pallas_call | solution.py:272
  40.4 0.0 copy-start
  40.4 1.7 %copy.14 = f32[512,128]{1,0:T(8,128)} copy(f32[512,128]{1,0:T(8,128)} %get-tuple-element.8) | data formatting | bytes 524288
  42.2 0.0 copy-done
  42.2 0.7 %copy.15 = f32[1,512,137]{1,0,2:T(1,128)} copy(f32[1,512,137]{1,0,2:T(1,128)S(1)} %bitcast.9) | data formatting | bytes 561152
Async XLA Ops:
  40.4 1.7 %copy-start = (f32[137,1,512]{2,1,0:T(1,128)S(1)}, f32[137,1,512]{2,1,0:T(1,128)}, u32[]{:S(2)}) copy-start(f32[137,1,512]{2,1,0:T(1,128)} %get-tuple-element.5) | copy-start | bytes 841732

commit v3 on v2

v3 whole, which is shorter than its diff:
```python
import functools

import jax
import jax.numpy as jnp
from jax import lax
from jax.experimental import pallas as pl
from jax.experimental.pallas import tpu as pltpu
from jax.sharding import PartitionSpec as P

MESH = pl.DeviceIdType.MESH
F32 = jnp.float32
BF16 = jnp.bfloat16

META, Z, RS, AG, BK = 0, 12, 22, 34, 46
COPIES = 56

LEFT, RIGHT, HEAD, TAIL = 0, 1, 2, 3


def nt(a, b):
    return lax.dot_general(a, b, (((1,), (1,)), ((), ())), preferred_element_type=F32)


def kernel(
    n_space, total_cols,
    state_in, start_in, w_in, slot_in, frac_in, count_ref, obs_in, jac_in, inv_in,
    dep_out, adj_out,
    state_ref, start_ref, w_ref, slot_ref, frac_ref, obs_ref, jac_ref, inv_ref,
    m_start, m_w, m_slot, m_frac, foot, zbuf, acc, abuf, pout, relay, rin, sbuf, wide, wout, win, rim, swap, obs_t, inv_t, dep_t,
    load, send, recv,
):
    t = lax.axis_index("tm")
    s = lax.axis_index("space")
    mate = t + 1 - 2 * lax.rem(t, 2)
    y1 = lax.rem(mate + 2, 8)
    y2 = lax.rem(t + 4, 8)
    y3 = lax.rem(mate + 6, 8)
    left = lax.rem(s + n_space - 1, n_space)
    right = lax.rem(s + 1, n_space)
    chans = 128
    quarter = 128
    top, bottom = pl.ds(0, 64), pl.ds(64, 64)

    barrier = pltpu.get_barrier_semaphore()
    for peer in ((t, right), (t, left), (mate, left), (mate, right), (y2, s), (y1, s), (y3, s), (mate, s)):
        pl.semaphore_signal(barrier, inc=1, device_id=peer, device_id_type=MESH)

    loads = [
        pltpu.make_async_copy(src, dst, load.at[k])
        for k, (src, dst) in enumerate(
            (
                (state_in, state_ref), (jac_in, jac_ref), (start_in, start_ref), (w_in, w_ref), (slot_in, slot_ref),
                (frac_in, frac_ref), (obs_in, obs_ref), (inv_in, inv_ref),
            )
        )
    ]
    for c in loads:
        c.start()

    def copy(index, src, dst, device):
        return pltpu.make_async_remote_copy(
            src_ref=src, dst_ref=dst, send_sem=send.at[index], recv_sem=recv.at[index],
            device_id=device, device_id_type=MESH,
        )

    loads[0].wait()
    loads[1].wait()
    z = lax.dot_general(jac_ref[...], state_ref[...], (((0,), (0,)), ((), ())), preferred_element_type=F32).astype(BF16)
    zbuf[HEAD, 0] = z[:, :256]
    zbuf[TAIL, 0] = z[:, 256:]
    for c in loads[2:6]:
        c.wait()

    pl.semaphore_wait(barrier, 8)

    sides = ((HEAD, RIGHT, left), (TAIL, LEFT, right))
    z_relayed = [copy(Z + k, zbuf.at[a, 0, top], zbuf.at[b, 0, top], (t, d)) for k, (a, b, d) in enumerate(sides)]
    z_direct = [copy(Z + 2 + k, zbuf.at[a, 0, bottom], zbuf.at[b, 0, bottom], (t, d)) for k, (a, b, d) in enumerate(sides)]
    z_cross = [copy(Z + 4 + k, zbuf.at[a, 0, bottom], zbuf.at[b, 1, bottom], (mate, d)) for k, (a, b, d) in enumerate(sides)]
    z_onward = [copy(Z + 6 + k, zbuf.at[b, 0, top], zbuf.at[b, 1, top], (mate, s)) for k, (a, b, d) in enumerate(sides)]
    z_mate = [copy(Z + 8 + k, zbuf.at[a, 0], zbuf.at[a, 1], (mate, s)) for k, (a, b, d) in enumerate(sides)]
    fields = ((start_ref, m_start), (w_ref, m_w), (slot_ref, m_slot), (frac_ref, m_frac))
    meta = {}
    for hop, peer in ((2, y2), (1, y1), (3, y3)):
        at = 3 - hop
        meta[at] = [copy(META + 4 * at + kind, src, dst.at[at], (peer, s)) for kind, (src, dst) in enumerate(fields)]
    for c in z_relayed + z_direct + z_cross + meta[1] + meta[2] + meta[0] + z_mate:
        c.start()

    def weight_of(slot, frac, held):
        return jnp.where(slot == held, 1.0 - frac, 0.0) + jnp.where(slot + 1 == held, frac, 0.0)

    def build(group, start, w, slot, frac):
        abuf[group, 0:1, :] = weight_of(slot, frac, t)
        abuf[group, 1:2, :] = weight_of(slot, frac, mate)
        local = jnp.bitwise_and(start - s * 512 + 256, total_cols - 1)
        row = lax.broadcasted_iota(jnp.int32, (8, 512), 0)
        ahead = jnp.bitwise_and(row - local, 7)
        weights = w.astype(F32)
        turned = jnp.zeros((8, 512), F32)
        for k in range(8):
            turned = turned + jnp.where(ahead == k, weights[k : k + 1, :], 0.0)
        block = lax.shift_right_arithmetic(local - row + 7, 3)

        for first, last, shift in ((0, 4, 0), (4, 8, 8), (8, 16, -4)):

            def rows(index, carry):
                parts = [jnp.where(block == (index + shift) * 8 + m, turned, 0.0) for m in range(8)]
                at = pl.ds(pl.multiple_of(index * 64, 64), 64)
                foot[group, at, :] = jnp.concatenate(parts, axis=0).astype(BF16)
                return carry

            lax.fori_loop(first, last, rows, 0)

    def columns(first):
        return jnp.concatenate(
            [
                jnp.concatenate([zbuf[first, 0], zbuf[first + 1, 0]], axis=1),
                jnp.concatenate([zbuf[first, 1], zbuf[first + 1, 1]], axis=1),
            ],
            axis=0,
        )

    def centre(group):
        acc[group] = jnp.dot(columns(HEAD), foot[group, 512:1024, :], preferred_element_type=F32)

    build(0, start_ref[...], w_ref[...], slot_ref[...], frac_ref[...])
    for c in loads[6:]:
        c.wait()
    obs_t[...] = jnp.transpose(obs_ref[...])
    inv_t[...] = jnp.transpose(jnp.broadcast_to(inv_ref[...], (chans, chans)))
    for c in z_mate:
        c.wait_recv()
    centre(0)
    for group in (1, 3):
        for c in meta[group - 1]:
            c.wait_recv()
        build(group, m_start[group - 1], m_w[group - 1], m_slot[group - 1], m_frac[group - 1])
        centre(group)
    for k in (1, 0):
        z_relayed[k].wait_recv()
        z_onward[k].start()
    for c in meta[1]:
        c.wait_recv()
    build(2, m_start[1], m_w[1], m_slot[1], m_frac[1])
    centre(2)
    for c in z_direct + z_onward + z_cross:
        c.wait_recv()

    def finish(group, half):
        span = slice(half * 256, (half + 1) * 256)
        total = acc[group, :, span] + jnp.dot(columns(LEFT), foot[group, 0:512, span], preferred_element_type=F32)
        return abuf[group, 0:1, span] * total[:chans] + abuf[group, 1:2, span] * total[chans:]

    def lanes(q):
        return slice(q * quarter, (q + 1) * quarter)

    far = [copy(RS + q, pout.at[q], relay.at[q], ((y1, y3)[q % 2], s)) for q in range(4)]
    to_next = [copy(RS + 4 + q, pout.at[4 + q], rin.at[0, q], (y1, s)) for q in range(4)]
    to_last = [copy(RS + 8 + q, pout.at[8 + q], rin.at[1, q], (y3, s)) for q in range(4)]
    for half in range(2):
        partial = finish(2, half)
        for k in range(2):
            pout[2 * half + k] = partial[:, lanes(k)].astype(BF16)
            far[2 * half + k].start()
    for half in range(2):
        for group, base, copies, now in ((1, 4, to_next, 1), (3, 8, to_last, 0)):
            partial = finish(group, half)
            q = 2 * half + now
            pout[base + q] = partial[:, lanes(now)].astype(BF16)
            copies[q].start()
            acc[group, 0:chans, lanes(q + 1 - 2 * now)] = partial[:, lanes(1 - now)]
    for half in range(2):
        acc[0, 0:chans, half * 256 : (half + 1) * 256] = finish(0, half)
    for q in range(4):
        group, base, copies = ((1, 4, to_next), (3, 8, to_last))[q % 2]
        far[q].wait_recv()
        pout[base + q] = (acc[group, 0:chans, lanes(q)] + relay[q].astype(F32)).astype(BF16)
        copies[q].start()

    ag_next = [copy(AG + q, sbuf.at[0, q], sbuf.at[3, q], (y1, s)) for q in range(4)]
    ag_last = [copy(AG + 4 + q, sbuf.at[0, q], sbuf.at[1, q], (y3, s)) for q in range(4)]
    ag_far = [
        copy(AG + 8 + q, sbuf.at[(3, 1)[q % 2], q], sbuf.at[2, q], ((y1, y3)[q % 2], s)) for q in range(4)
    ]
    column = lax.broadcasted_iota(jnp.int32, (1, quarter), 1)
    for q in range(4):
        to_next[q].wait_recv()
        to_last[q].wait_recv()
        projected = acc[0, 0:chans, lanes(q)] + rin[0, q].astype(F32) + rin[1, q].astype(F32)
        live = column + q * quarter < count_ref[0, 0]
        departed = jnp.where(live, obs_t[:, lanes(q)] - projected, 0.0)
        dep_t[:, lanes(q)] = departed
        sbuf[0, q] = (departed * inv_t[:, 0:1]).astype(BF16)
        (ag_next, ag_last)[q % 2][q].start()
    for q in (0, 2):
        ag_next[q + 1].start()
        ag_last[q].start()

    dep_out[...] = jnp.transpose(dep_t[...])

    def lanes_of(ref, group, rows, quarters):
        if quarters[-1] - quarters[0] == len(quarters) - 1:
            return ref[group, rows, quarters[0] * quarter : (quarters[-1] + 1) * quarter]
        return jnp.concatenate([ref[group, rows, lanes(q)] for q in quarters], axis=1)

    def by_slot(pieces):
        parts = []
        for slot in range(2):
            row = []
            for group, quarters in pieces:
                values = jnp.concatenate([sbuf[group, q] for q in quarters], axis=1).astype(F32)
                row.append((lanes_of(abuf, group, slice(slot, slot + 1), quarters) * values).astype(BF16))
            parts.append(jnp.concatenate(row, axis=1))
        return jnp.concatenate(parts, axis=0)

    def sums(v, pieces, chunk):
        rows = slice(chunk * 256, (chunk + 1) * 256)
        return nt(v, jnp.concatenate([lanes_of(foot, group, rows, quarters) for group, quarters in pieces], axis=1))

    def spread(*pieces, fresh=False):
        v = by_slot(pieces)
        for chunk in range(4):
            if fresh:
                wide[chunk] = sums(v, pieces, chunk)
            else:
                wide[chunk] += sums(v, pieces, chunk)

    spread((0, (0, 1, 2, 3)), fresh=True)
    for q in range(4):
        (ag_next, ag_last)[q % 2][q].wait_recv()
        ag_far[q].start()
    spread((3, (0, 2)), (1, (1, 3)))
    for c in (ag_next[1], ag_last[0], ag_next[3], ag_last[2]):
        c.wait_recv()
    spread((3, (1, 3)), (1, (0, 2)))
    ag_far[0].wait_recv()
    ag_far[1].wait_recv()
    spread((2, (0, 1)))
    ag_far[2].wait_recv()
    ag_far[3].wait_recv()
    ends = ((LEFT, left), (RIGHT, right))
    r_own = [copy(BK + k, wout.at[k, 0, top], rim.at[1 - k, 0], (t, d)) for k, d in ends]
    r_other = [copy(BK + 2 + k, wout.at[k, 1, top], rim.at[1 - k, 1], (mate, d)) for k, d in ends]
    r_swap = [copy(BK + 4 + k, wout.at[k, 0, bottom], swap.at[k], (mate, s)) for k, d in ends]
    r_sum = [copy(BK + 6 + k, wout.at[k, 1, bottom], rim.at[1 - k, 2], (mate, d)) for k, d in ends]
    r_mate = [copy(BK + 8 + k, wout.at[2 + k, 1], win.at[k], (mate, s)) for k in range(2)]
    last = ((2, (2, 3)),)
    v = by_slot(last)
    for k in (LEFT, RIGHT):
        total = wide[k] + sums(v, last, k)
        wide[k] = total
        wout[k, 0] = total[:chans].astype(BF16)
        wout[k, 1, 0:64] = total[chans : chans + 64].astype(BF16)
        r_swap[k].start()
        r_own[k].start()
        r_other[k].start()
    for k in range(2):
        total = wide[HEAD + k] + sums(v, last, HEAD + k)
        wide[HEAD + k] = total
        wout[2 + k, 1] = total[chans:].astype(BF16)
        r_mate[k].start()
    for k in (LEFT, RIGHT):
        r_swap[k].wait_recv()
        wout[k, 1, 64:128] = (wide[k, chans + 64 : 2 * chans] + swap[k].astype(F32)).astype(BF16)
        r_sum[k].start()
    for c in r_mate:
        c.wait_recv()
    for h in (1, 0):
        for c in (r_own[1 - h], r_other[1 - h], r_sum[1 - h]):
            c.wait_recv()
        rims = jnp.concatenate([rim[h, 0].astype(F32) + rim[h, 1].astype(F32), rim[h, 2].astype(F32)], axis=0)
        whole = wide[HEAD + h, 0:chans] + win[h].astype(F32) + rims
        adj_out[:, 0, h * 256 : (h + 1) * 256] = jnp.dot(jac_ref[...], whole.astype(BF16), preferred_element_type=F32)
    for group in (
        z_relayed, z_direct, z_cross, z_onward, z_mate, meta[0], meta[1], meta[2], far, to_next, to_last, ag_next, ag_last,
        ag_far, r_own, r_other, r_swap, r_sum, r_mate,
    ):
        for c in group:
            c.wait_send()


def body(state, obs_start, foot_weight, obs_slot, obs_frac, live_count, obs_values, jacobian, inv_var):
    n_space = lax.axis_size("space")
    levels = jacobian.shape[0]
    anywhere = pl.BlockSpec(memory_space=pl.ANY)
    vmem = pl.BlockSpec(memory_space=pltpu.VMEM)
    i32 = jnp.int32
    departures, adjoint = pl.pallas_call(
        functools.partial(kernel, n_space, 512 * n_space),
        out_shape=(
            pltpu.VMEM((512, 128), F32),
            pltpu.VMEM((levels, 1, 512), F32),
        ),
        in_specs=[anywhere] * 5 + [pl.BlockSpec(memory_space=pltpu.SMEM)] + [anywhere] * 3,
        out_specs=(vmem, vmem),
        scratch_shapes=[
            pltpu.VMEM((levels, 512), BF16),
            pltpu.VMEM((1, 512), i32),
            pltpu.VMEM((8, 512), BF16),
            pltpu.VMEM((1, 512), i32),
            pltpu.VMEM((1, 512), F32),
            pltpu.VMEM((512, 128), F32),
            pltpu.VMEM((levels, 128), BF16),
            pltpu.VMEM((1, 128), F32),
            pltpu.VMEM((3, 1, 512), i32),
            pltpu.VMEM((3, 8, 512), BF16),
            pltpu.VMEM((3, 1, 512), i32),
            pltpu.VMEM((3, 1, 512), F32),
            pltpu.VMEM((4, 1024, 512), BF16),
            pltpu.VMEM((4, 2, 128, 256), BF16),
            pltpu.VMEM((4, 256, 512), F32),
            pltpu.VMEM((4, 2, 512), F32),
            pltpu.VMEM((12, 128, 128), BF16),
            pltpu.VMEM((4, 128, 128), BF16),
            pltpu.VMEM((2, 4, 128, 128), BF16),
            pltpu.VMEM((4, 4, 128, 128), BF16),
            pltpu.VMEM((4, 256, 256), F32),
            pltpu.VMEM((4, 2, 128, 256), BF16),
            pltpu.VMEM((2, 128, 256), BF16),
            pltpu.VMEM((2, 3, 64, 256), BF16),
            pltpu.VMEM((2, 64, 256), BF16),
            pltpu.VMEM((128, 512), F32),
            pltpu.VMEM((128, 128), F32),
            pltpu.VMEM((128, 512), F32),
            pltpu.SemaphoreType.DMA((8,)),
            pltpu.SemaphoreType.DMA((COPIES,)),
            pltpu.SemaphoreType.DMA((COPIES,)),
        ],
        compiler_params=pltpu.CompilerParams(collective_id=0, has_side_effects=True),
        name="window",
    )(
        jnp.transpose(state[0]),
        obs_start[None],
        jnp.transpose(foot_weight),
        obs_slot[None],
        obs_frac[None],
        live_count,
        obs_values,
        jacobian,
        inv_var[None],
    )
    return departures, jnp.transpose(adjoint, (1, 2, 0))


def solution(mesh):
    return jax.shard_map(
        body,
        mesh=mesh,
        in_specs=(
            P("tm", "space", None),
            P(("tm", "space")),
            P(("tm", "space"), None),
            P(("tm", "space")),
            P(("tm", "space")),
            P("tm", "space"),
            P(("tm", "space"), None),
            P(),
            P(),
        ),
        out_specs=(P(("tm", "space"), None), P("tm", "space", None)),
        check_vma=False,
    )
```

time: 43 us -> 40.1 us (0.933)
  Pallas kernels: 39.2 us -> 37.3 us
  local copies, waits for them, and re-layouts: 2.43 us -> 1.41 us
    pallas_call x1, Pallas kernels: 39.2 us -> 37.3 us  [body(): pl.pallas_call(functools.partial(kernel, n_space, 512 * n_space), out_sha...]
    unnamed x4 -> x2, local copies, waits for them, and re-layouts: 2.43 us -> 1.41 us
where the time goes in v3:
time: 40.1 us; the launch traced here: 40 us
  Pallas kernels  37.3 us (93%)
  local copies, waits for them, and re-layouts  1.41 us (4%)
  between operations  1.29 us (3%)
    pallas_call x1, Pallas kernels, body(): pl.pallas_call(functools.partial(kernel, n_space, 512 * n_space), out_sha...  37.3 us
    unnamed x2, local copies, waits for them, and re-layouts  1.41 us

profile of v3, /device:TPU:1, one launch (start us, length us, event | category | flops | bytes accessed | tf_op | source)
XLA Modules:
  0.0 40.0 jit_solution(3866514235656480798)
XLA Ops:
  1.3 37.3 %window.1 = (f32[512,128]{1,0:T(8,128)S(1)}, f32[137,1,512]{2,1,0:T(1,128)S(1)}) custom-call(bf16[137,512]{1,0:T(8,128)(2,1)} %bitcast.10, s32[1,512]{1,0:T(1,128)} %bitcast.12, bf16[8,512]{1,0:T(8,128)(2,1)} %bitcast.11, s32[1,512]{1,0:T(1,128)} %bitcast.13, f32[1,512]{1,0:T(1,128)} %bitcast.14, s32[1,1]{1,0:T(1,128)S(6)} %copy.15.count_ref, ...), custom_call_target="tpu_custom_call" | custom-call | tf_op jit(solution)/shard_map/window/pallas_call | solution.py:289
  38.6 0.7 %copy.13 = f32[512,128]{1,0:T(8,128)} copy(f32[512,128]{1,0:T(8,128)S(1)} %get-tuple-element.6) | data formatting | bytes 524288
  39.3 0.7 %copy.14 = f32[1,512,137]{1,0,2:T(1,128)} copy(f32[1,512,137]{1,0,2:T(1,128)S(1)} %bitcast.9) | data formatting | bytes 561152

commit v4 on v3

--- a/solution.py
+++ b/solution.py
@@ -11,8 +11,8 @@
 F32 = jnp.float32
 BF16 = jnp.bfloat16
 
-META, Z, RS, AG, BK = 0, 12, 22, 34, 46
-COPIES = 56
+META, Z_MATE, Z_RELAYED, Z_REST, FAR, SUM, FIRST, SECOND, LAST, SWAP, RIMS = 0, 3, 4, 6, 7, 11, 15, 19, 20, 22, 24
+ARRIVALS = 25
 
 LEFT, RIGHT, HEAD, TAIL = 0, 1, 2, 3
 
@@ -26,7 +26,7 @@
     state_in, start_in, w_in, slot_in, frac_in, count_ref, obs_in, jac_in, inv_in,
     dep_out, adj_out,
     state_ref, start_ref, w_ref, slot_ref, frac_ref, obs_ref, jac_ref, inv_ref,
-    m_start, m_w, m_slot, m_frac, foot, zbuf, acc, abuf, pout, relay, rin, sbuf, wide, wout, win, rim, swap, obs_t, inv_t, dep_t,
+    o_pack, m_pack, m_w, foot, zbuf, acc, abuf, pout, relay, rin, sbuf, wide, wout, win, rim, swap, obs_t, inv_t, dep_t,
     load, send, recv,
 ):
     t = lax.axis_index("tm")
@@ -59,9 +59,12 @@
 
     def copy(index, src, dst, device):
         return pltpu.make_async_remote_copy(
-            src_ref=src, dst_ref=dst, send_sem=send.at[index], recv_sem=recv.at[index],
+            src_ref=src, dst_ref=dst, send_sem=send.at[0], recv_sem=recv.at[index],
             device_id=device, device_id_type=MESH,
         )
+
+    def arrived(index, ref):
+        copy(index, ref, ref, (mate, s)).wait_recv()
 
     loads[0].wait()
     loads[1].wait()
@@ -70,20 +73,24 @@
     zbuf[TAIL, 0] = z[:, 256:]
     for c in loads[2:6]:
         c.wait()
+    o_pack[0] = start_ref[...].astype(F32)
+    o_pack[1] = slot_ref[...].astype(F32)
+    o_pack[2] = frac_ref[...]
+    o_pack[3] = jnp.zeros((1, 512), F32)
 
     pl.semaphore_wait(barrier, 8)
 
     sides = ((HEAD, RIGHT, left), (TAIL, LEFT, right))
-    z_relayed = [copy(Z + k, zbuf.at[a, 0, top], zbuf.at[b, 0, top], (t, d)) for k, (a, b, d) in enumerate(sides)]
-    z_direct = [copy(Z + 2 + k, zbuf.at[a, 0, bottom], zbuf.at[b, 0, bottom], (t, d)) for k, (a, b, d) in enumerate(sides)]
-    z_cross = [copy(Z + 4 + k, zbuf.at[a, 0, bottom], zbuf.at[b, 1, bottom], (mate, d)) for k, (a, b, d) in enumerate(sides)]
-    z_onward = [copy(Z + 6 + k, zbuf.at[b, 0, top], zbuf.at[b, 1, top], (mate, s)) for k, (a, b, d) in enumerate(sides)]
-    z_mate = [copy(Z + 8 + k, zbuf.at[a, 0], zbuf.at[a, 1], (mate, s)) for k, (a, b, d) in enumerate(sides)]
-    fields = ((start_ref, m_start), (w_ref, m_w), (slot_ref, m_slot), (frac_ref, m_frac))
+    z_relayed = [copy(Z_RELAYED + k, zbuf.at[a, 0, top], zbuf.at[b, 0, top], (t, d)) for k, (a, b, d) in enumerate(sides)]
+    z_direct = [copy(Z_REST, zbuf.at[a, 0, bottom], zbuf.at[b, 0, bottom], (t, d)) for a, b, d in sides]
+    z_cross = [copy(Z_REST, zbuf.at[a, 0, bottom], zbuf.at[b, 1, bottom], (mate, d)) for a, b, d in sides]
+    z_onward = [copy(Z_REST, zbuf.at[b, 0, top], zbuf.at[b, 1, top], (mate, s)) for a, b, d in sides]
+    z_mate = [copy(Z_MATE, zbuf.at[a, 0], zbuf.at[a, 1], (mate, s)) for a, b, d in sides]
+    fields = ((o_pack, m_pack), (w_ref, m_w))
     meta = {}
     for hop, peer in ((2, y2), (1, y1), (3, y3)):
         at = 3 - hop
-        meta[at] = [copy(META + 4 * at + kind, src, dst.at[at], (peer, s)) for kind, (src, dst) in enumerate(fields)]
+        meta[at] = [copy(META + at, src, dst.at[at], (peer, s)) for src, dst in fields]
     for c in z_relayed + z_direct + z_cross + meta[1] + meta[2] + meta[0] + z_mate:
         c.start()
 
@@ -124,69 +131,64 @@
     def centre(group):
         acc[group] = jnp.dot(columns(HEAD), foot[group, 512:1024, :], preferred_element_type=F32)
 
+    def gathered(group):
+        at = group - 1
+        arrived(META + at, foot.at[group, 0:16])
+        build(group, m_pack[at, 0].astype(jnp.int32), m_w[at], m_pack[at, 1].astype(jnp.int32), m_pack[at, 2])
+
     build(0, start_ref[...], w_ref[...], slot_ref[...], frac_ref[...])
     for c in loads[6:]:
         c.wait()
     obs_t[...] = jnp.transpose(obs_ref[...])
     inv_t[...] = jnp.transpose(jnp.broadcast_to(inv_ref[...], (chans, chans)))
-    for c in z_mate:
-        c.wait_recv()
+    arrived(Z_MATE, zbuf.at[HEAD : HEAD + 2, 1])
     centre(0)
     for group in (1, 3):
-        for c in meta[group - 1]:
-            c.wait_recv()
-        build(group, m_start[group - 1], m_w[group - 1], m_slot[group - 1], m_frac[group - 1])
+        gathered(group)
         centre(group)
     for k in (1, 0):
         z_relayed[k].wait_recv()
         z_onward[k].start()
-    for c in meta[1]:
-        c.wait_recv()
-    build(2, m_start[1], m_w[1], m_slot[1], m_frac[1])
+    gathered(2)
     centre(2)
-    for c in z_direct + z_onward + z_cross:
-        c.wait_recv()
-
-    def finish(group, half):
-        span = slice(half * 256, (half + 1) * 256)
-        total = acc[group, :, span] + jnp.dot(columns(LEFT), foot[group, 0:512, span], preferred_element_type=F32)
-        return abuf[group, 0:1, span] * total[:chans] + abuf[group, 1:2, span] * total[chans:]
+    arrived(Z_REST, zbuf.at[0:3, 0])
+
+    def finish(group):
+        total = acc[group] + jnp.dot(columns(LEFT), foot[group, 0:512, :], preferred_element_type=F32)
+        return abuf[group, 0:1, :] * total[:chans] + abuf[group, 1:2, :] * total[chans:]
 
     def lanes(q):
         return slice(q * quarter, (q + 1) * quarter)
 
-    far = [copy(RS + q, pout.at[q], relay.at[q], ((y1, y3)[q % 2], s)) for q in range(4)]
-    to_next = [copy(RS + 4 + q, pout.at[4 + q], rin.at[0, q], (y1, s)) for q in range(4)]
-    to_last = [copy(RS + 8 + q, pout.at[8 + q], rin.at[1, q], (y3, s)) for q in range(4)]
-    for half in range(2):
-        partial = finish(2, half)
-        for k in range(2):
-            pout[2 * half + k] = partial[:, lanes(k)].astype(BF16)
-            far[2 * half + k].start()
-    for half in range(2):
-        for group, base, copies, now in ((1, 4, to_next, 1), (3, 8, to_last, 0)):
-            partial = finish(group, half)
-            q = 2 * half + now
-            pout[base + q] = partial[:, lanes(now)].astype(BF16)
+    far = [copy(FAR + q, pout.at[q], relay.at[q], ((y1, y3)[q % 2], s)) for q in range(4)]
+    to_next = [copy(SUM + q, pout.at[4 + q], rin.at[0, q], (y1, s)) for q in range(4)]
+    to_last = [copy(SUM + q, pout.at[8 + q], rin.at[1, q], (y3, s)) for q in range(4)]
+    partial = finish(2)
+    for q in range(4):
+        pout[q] = partial[:, lanes(q)].astype(BF16)
+        far[q].start()
+    for group, base, copies, now in ((1, 4, to_next, 1), (3, 8, to_last, 0)):
+        partial = finish(group)
+        for q in (now, now + 2):
+            pout[base + q] = partial[:, lanes(q)].astype(BF16)
             copies[q].start()
-            acc[group, 0:chans, lanes(q + 1 - 2 * now)] = partial[:, lanes(1 - now)]
-    for half in range(2):
-        acc[0, 0:chans, half * 256 : (half + 1) * 256] = finish(0, half)
+        for q in (1 - now, 3 - now):
+            acc[group, 0:chans, lanes(q)] = partial[:, lanes(q)]
+    acc[0, 0:chans] = finish(0)
     for q in range(4):
         group, base, copies = ((1, 4, to_next), (3, 8, to_last))[q % 2]
         far[q].wait_recv()
         pout[base + q] = (acc[group, 0:chans, lanes(q)] + relay[q].astype(F32)).astype(BF16)
         copies[q].start()
 
-    ag_next = [copy(AG + q, sbuf.at[0, q], sbuf.at[3, q], (y1, s)) for q in range(4)]
-    ag_last = [copy(AG + 4 + q, sbuf.at[0, q], sbuf.at[1, q], (y3, s)) for q in range(4)]
+    ag_next = [copy(FIRST + q if q % 2 == 0 else SECOND, sbuf.at[0, q], sbuf.at[3, q], (y1, s)) for q in range(4)]
+    ag_last = [copy(FIRST + q if q % 2 else SECOND, sbuf.at[0, q], sbuf.at[1, q], (y3, s)) for q in range(4)]
     ag_far = [
-        copy(AG + 8 + q, sbuf.at[(3, 1)[q % 2], q], sbuf.at[2, q], ((y1, y3)[q % 2], s)) for q in range(4)
+        copy(LAST + q // 2, sbuf.at[(3, 1)[q % 2], q], sbuf.at[2, q], ((y1, y3)[q % 2], s)) for q in range(4)
     ]
     column = lax.broadcasted_iota(jnp.int32, (1, quarter), 1)
     for q in range(4):
-        to_next[q].wait_recv()
-        to_last[q].wait_recv()
+        arrived(SUM + q, rin.at[:, q])
         projected = acc[0, 0:chans, lanes(q)] + rin[0, q].astype(F32) + rin[1, q].astype(F32)
         live = column + q * quarter < count_ref[0, 0]
         departed = jnp.where(live, obs_t[:, lanes(q)] - projected, 0.0)
@@ -231,20 +233,17 @@
         (ag_next, ag_last)[q % 2][q].wait_recv()
         ag_far[q].start()
     spread((3, (0, 2)), (1, (1, 3)))
-    for c in (ag_next[1], ag_last[0], ag_next[3], ag_last[2]):
-        c.wait_recv()
+    arrived(SECOND, sbuf.at[3])
     spread((3, (1, 3)), (1, (0, 2)))
-    ag_far[0].wait_recv()
-    ag_far[1].wait_recv()
+    arrived(LAST, sbuf.at[2, 0:2])
     spread((2, (0, 1)))
-    ag_far[2].wait_recv()
-    ag_far[3].wait_recv()
+    arrived(LAST + 1, sbuf.at[2, 2:4])
     ends = ((LEFT, left), (RIGHT, right))
-    r_own = [copy(BK + k, wout.at[k, 0, top], rim.at[1 - k, 0], (t, d)) for k, d in ends]
-    r_other = [copy(BK + 2 + k, wout.at[k, 1, top], rim.at[1 - k, 1], (mate, d)) for k, d in ends]
-    r_swap = [copy(BK + 4 + k, wout.at[k, 0, bottom], swap.at[k], (mate, s)) for k, d in ends]
-    r_sum = [copy(BK + 6 + k, wout.at[k, 1, bottom], rim.at[1 - k, 2], (mate, d)) for k, d in ends]
-    r_mate = [copy(BK + 8 + k, wout.at[2 + k, 1], win.at[k], (mate, s)) for k in range(2)]
+    r_own = [copy(RIMS, wout.at[k, 0, top], rim.at[1 - k, 0], (t, d)) for k, d in ends]
+    r_other = [copy(RIMS, wout.at[k, 1, top], rim.at[1 - k, 1], (mate, d)) for k, d in ends]
+    r_swap = [copy(SWAP + k, wout.at[k, 0, bottom], swap.at[k], (mate, s)) for k, d in ends]
+    r_sum = [copy(RIMS, wout.at[k, 1, bottom], rim.at[1 - k, 2], (mate, d)) for k, d in ends]
+    r_mate = [copy(RIMS, wout.at[2 + k, 1], win.at[k], (mate, s)) for k in range(2)]
     last = ((2, (2, 3)),)
     v = by_slot(last)
     for k in (LEFT, RIGHT):
@@ -264,20 +263,21 @@
         r_swap[k].wait_recv()
         wout[k, 1, 64:128] = (wide[k, chans + 64 : 2 * chans] + swap[k].astype(F32)).astype(BF16)
         r_sum[k].start()
-    for c in r_mate:
-        c.wait_recv()
-    for h in (1, 0):
-        for c in (r_own[1 - h], r_other[1 - h], r_sum[1 - h]):
-            c.wait_recv()
+    arrived(RIMS, pout.at[0:10])
+    for h in range(2):
         rims = jnp.concatenate([rim[h, 0].astype(F32) + rim[h, 1].astype(F32), rim[h, 2].astype(F32)], axis=0)
         whole = wide[HEAD + h, 0:chans] + win[h].astype(F32) + rims
         adj_out[:, 0, h * 256 : (h + 1) * 256] = jnp.dot(jac_ref[...], whole.astype(BF16), preferred_element_type=F32)
-    for group in (
-        z_relayed, z_direct, z_cross, z_onward, z_mate, meta[0], meta[1], meta[2], far, to_next, to_last, ag_next, ag_last,
-        ag_far, r_own, r_other, r_swap, r_sum, r_mate,
-    ):
-        for c in group:
-            c.wait_send()
+    sent = foot.at[0:3, 0:528]
+    copy(META, sent, sent, (mate, s)).wait_send()
+
+
+def write(dep_in, adj_in, dep_out, adj_out, done):
+    copies = [pltpu.make_async_copy(dep_in, dep_out, done.at[0]), pltpu.make_async_copy(adj_in, adj_out, done.at[1])]
+    for c in copies:
+        c.start()
+    for c in copies:
+        c.wait()
 
 
 def body(state, obs_start, foot_weight, obs_slot, obs_frac, live_count, obs_values, jacobian, inv_var):
@@ -303,10 +303,9 @@
             pltpu.VMEM((512, 128), F32),
             pltpu.VMEM((levels, 128), BF16),
             pltpu.VMEM((1, 128), F32),
-            pltpu.VMEM((3, 1, 512), i32),
+            pltpu.VMEM((4, 1, 512), F32),
+            pltpu.VMEM((3, 4, 1, 512), F32),
             pltpu.VMEM((3, 8, 512), BF16),
-            pltpu.VMEM((3, 1, 512), i32),
-            pltpu.VMEM((3, 1, 512), F32),
             pltpu.VMEM((4, 1024, 512), BF16),
             pltpu.VMEM((4, 2, 128, 256), BF16),
             pltpu.VMEM((4, 256, 512), F32),
@@ -324,8 +323,8 @@
             pltpu.VMEM((128, 128), F32),
             pltpu.VMEM((128, 512), F32),
             pltpu.SemaphoreType.DMA((8,)),
-            pltpu.SemaphoreType.DMA((COPIES,)),
-            pltpu.SemaphoreType.DMA((COPIES,)),
+            pltpu.SemaphoreType.DMA((1,)),
+            pltpu.SemaphoreType.DMA((ARRIVALS,)),
         ],
         compiler_params=pltpu.CompilerParams(collective_id=0, has_side_effects=True),
         name="window",
@@ -340,6 +339,14 @@
         jacobian,
         inv_var[None],
     )
+    departures, adjoint = pl.pallas_call(
+        write,
+        out_shape=(jax.ShapeDtypeStruct(departures.shape, F32), jax.ShapeDtypeStruct(adjoint.shape, F32)),
+        in_specs=[vmem] * 2,
+        out_specs=(anywhere, anywhere),
+        scratch_shapes=[pltpu.SemaphoreType.DMA((2,))],
+        name="write",
+    )(pltpu.with_memory_space_constraint(departures, pltpu.VMEM), pltpu.with_memory_space_constraint(adjoint, pltpu.VMEM))
     return departures, jnp.transpose(adjoint, (1, 2, 0))
 
 

time: 40.1 us -> 38.7 us (0.965)
  local copies, waits for them, and re-layouts: 1.41 us -> 0 us
    unnamed x2 -> x0, local copies, waits for them, and re-layouts: 1.41 us -> none
    pallas_call x0 -> x1, Pallas kernels: none -> 0.81 us  [body(): pl.pallas_call(write, out_shape=(jax.ShapeDtypeStruct(departures.shape, F...]
    pallas_call x1, Pallas kernels: 37.3 us -> 36.5 us  [body(): pl.pallas_call(functools.partial(kernel, n_space, 512 * n_space), out_sha...]
where the time goes in v4:
time: 38.7 us; the launch traced here: 38.6 us
  Pallas kernels  37.3 us (96%)
  between operations  1.29 us (3%)
    pallas_call x1, Pallas kernels, body(): pl.pallas_call(functools.partial(kernel, n_space, 512 * n_space), out_sha...  36.5 us
    pallas_call x1, Pallas kernels, body(): pl.pallas_call(write, out_shape=(jax.ShapeDtypeStruct(departures.shape, F...  0.81 us

profile of v4, /device:TPU:1, one launch (start us, length us, event | category | flops | bytes accessed | tf_op | source)
XLA Modules:
  0.0 38.6 jit_solution(15787875286611030430)
XLA Ops:
  1.3 36.5 %window.1 = (f32[512,128]{1,0:T(8,128)S(1)}, f32[137,1,512]{2,1,0:T(1,128)S(1)}) custom-call(bf16[137,512]{1,0:T(8,128)(2,1)} %bitcast.9, s32[1,512]{1,0:T(1,128)} %bitcast.11, bf16[8,512]{1,0:T(8,128)(2,1)} %bitcast.10, s32[1,512]{1,0:T(1,128)} %bitcast.12, f32[1,512]{1,0:T(1,128)} %bitcast.13, s32[1,1]{1,0:T(1,128)S(6)} %copy.11.count_ref, ...), custom_call_target="tpu_custom_call" | custom-call | tf_op jit(solution)/shard_map/window/pallas_call | solution.py:289
  37.8 0.8 %write.1 = (f32[512,128]{1,0:T(8,128)}, f32[137,1,512]{2,1,0:T(1,128)}) custom-call(f32[512,128]{1,0:T(8,128)S(1)} %get-tuple-element.6.dep_in, f32[137,1,512]{2,1,0:T(1,128)S(1)} %get-tuple-element.7.adj_in), custom_call_target="tpu_custom_call" | custom-call | tf_op jit(solution)/shard_map/write/pallas_call | solution.py:342

commit v5 on v4

--- a/solution.py
+++ b/solution.py
@@ -11,8 +11,8 @@
 F32 = jnp.float32
 BF16 = jnp.bfloat16
 
-META, Z_MATE, Z_RELAYED, Z_REST, FAR, SUM, FIRST, SECOND, LAST, SWAP, RIMS = 0, 3, 4, 6, 7, 11, 15, 19, 20, 22, 24
-ARRIVALS = 25
+META, Z_MATE, Z_RELAYED, Z_REST, FAR, SUM, FIRST, SECOND, LAST, SWAP, RIMS, HELD = 0, 3, 4, 6, 7, 11, 15, 19, 20, 22, 24, 25
+ARRIVALS = 26
 
 LEFT, RIGHT, HEAD, TAIL = 0, 1, 2, 3
 
@@ -22,12 +22,12 @@
 
 
 def kernel(
-    n_space, total_cols,
+    n_space, total_cols, holder,
     state_in, start_in, w_in, slot_in, frac_in, count_ref, obs_in, jac_in, inv_in,
     dep_out, adj_out,
     state_ref, start_ref, w_ref, slot_ref, frac_ref, obs_ref, jac_ref, inv_ref,
-    o_pack, m_pack, m_w, foot, zbuf, acc, abuf, pout, relay, rin, sbuf, wide, wout, win, rim, swap, obs_t, inv_t, dep_t,
-    load, send, recv,
+    o_pack, m_pack, m_w, held, foot, zbuf, acc, abuf, pout, relay, rin, sbuf, wide, wout, win, rim, swap, obs_t, inv_t, dep_t,
+    load, send, recv, gate,
 ):
     t = lax.axis_index("tm")
     s = lax.axis_index("space")
@@ -41,9 +41,35 @@
     quarter = 128
     top, bottom = pl.ds(0, 64), pl.ds(64, 64)
 
+    core = lax.rem(t, 2)
+    first_core, second_core = t - core, t - core + 1
+    is_zero, is_last, is_holder = s == 0, s == n_space - 1, s == holder
+    is_keeper = jnp.logical_and(is_holder, core == 1)
+
     barrier = pltpu.get_barrier_semaphore()
-    for peer in ((t, right), (t, left), (mate, left), (mate, right), (y2, s), (y1, s), (y3, s), (mate, s)):
-        pl.semaphore_signal(barrier, inc=1, device_id=peer, device_id_type=MESH)
+
+    def greet(core_index, tile):
+        pl.semaphore_signal(barrier, inc=1, device_id=(core_index, tile), device_id_type=MESH)
+
+    for peer in (t, mate):
+        goes_on = jnp.where(is_last, 1, 0)
+        to_holder = jnp.where(right == holder, 1, 0)
+        normal = peer - to_holder * lax.rem(peer, 2)
+        greet(goes_on * second_core + (1 - goes_on) * normal, goes_on * holder + (1 - goes_on) * right)
+    for peer in (t, mate):
+        greet(peer - jnp.where(left == holder, 1, 0) * lax.rem(peer, 2), left)
+    for peer in (y2, y1, y3):
+        greet(peer - jnp.where(is_holder, 1, 0) * lax.rem(peer, 2), s)
+    greet(mate, s)
+
+    @pl.when(is_zero)
+    def _():
+        greet(second_core, holder)
+
+    @pl.when(is_holder)
+    def _():
+        greet(t, 0)
+        greet(mate, 0)
 
     loads = [
         pltpu.make_async_copy(src, dst, load.at[k])
@@ -57,9 +83,9 @@
     for c in loads:
         c.start()
 
-    def copy(index, src, dst, device):
+    def copy(index, src, dst, device, out=0):
         return pltpu.make_async_remote_copy(
-            src_ref=src, dst_ref=dst, send_sem=send.at[0], recv_sem=recv.at[index],
+            src_ref=src, dst_ref=dst, send_sem=send.at[out], recv_sem=recv.at[index],
             device_id=device, device_id_type=MESH,
         )
 
@@ -78,20 +104,50 @@
     o_pack[2] = frac_ref[...]
     o_pack[3] = jnp.zeros((1, 512), F32)
 
-    pl.semaphore_wait(barrier, 8)
+    @pl.when(jnp.logical_not(is_keeper))
+    def _():
+        pl.semaphore_wait(barrier, 8 + 7 * jnp.where(is_holder, 1, 0))
+
+    @pl.when(jnp.logical_and(is_holder, core == 0))
+    def _():
+        pl.semaphore_signal(gate, inc=1, device_id=(mate, s), device_id_type=MESH)
+
+    @pl.when(is_keeper)
+    def _():
+        pl.semaphore_wait(gate, 1)
 
     sides = ((HEAD, RIGHT, left), (TAIL, LEFT, right))
-    z_relayed = [copy(Z_RELAYED + k, zbuf.at[a, 0, top], zbuf.at[b, 0, top], (t, d)) for k, (a, b, d) in enumerate(sides)]
-    z_direct = [copy(Z_REST, zbuf.at[a, 0, bottom], zbuf.at[b, 0, bottom], (t, d)) for a, b, d in sides]
-    z_cross = [copy(Z_REST, zbuf.at[a, 0, bottom], zbuf.at[b, 1, bottom], (mate, d)) for a, b, d in sides]
+    z_relayed = [copy(Z_RELAYED + k, zbuf.at[a, 0, top], zbuf.at[b, 0, top], (t, d), 1 - k) for k, (a, b, d) in enumerate(sides)]
+    z_direct = [copy(Z_REST, zbuf.at[a, 0, bottom], zbuf.at[b, 0, bottom], (t, d), 1 - k) for k, (a, b, d) in enumerate(sides)]
+    z_cross = [copy(Z_REST, zbuf.at[a, 0, bottom], zbuf.at[b, 1, bottom], (mate, d), 1 - k) for k, (a, b, d) in enumerate(sides)]
     z_onward = [copy(Z_REST, zbuf.at[b, 0, top], zbuf.at[b, 1, top], (mate, s)) for a, b, d in sides]
     z_mate = [copy(Z_MATE, zbuf.at[a, 0], zbuf.at[a, 1], (mate, s)) for a, b, d in sides]
+    z_held = [copy(HELD, zbuf.at[HEAD, k], held.at[k], (t, holder), 1) for k in range(2)]
+    last = n_space - 1
+    z_passed = [
+        copy(Z_RELAYED, held.at[1, top], zbuf.at[RIGHT, 0, top], (mate, last), 2),
+        copy(Z_RELAYED, held.at[0, top], zbuf.at[RIGHT, 0, top], (t, last), 2),
+        copy(Z_REST, held.at[1, bottom], zbuf.at[RIGHT, 0, bottom], (mate, last), 2),
+        copy(Z_REST, held.at[0, bottom], zbuf.at[RIGHT, 1, bottom], (mate, last), 2),
+        copy(Z_REST, held.at[0, bottom], zbuf.at[RIGHT, 0, bottom], (t, last), 2),
+        copy(Z_REST, held.at[1, bottom], zbuf.at[RIGHT, 1, bottom], (t, last), 2),
+    ]
+    sends_ahead = jnp.logical_and(is_zero, core == 1)
     fields = ((o_pack, m_pack), (w_ref, m_w))
     meta = {}
     for hop, peer in ((2, y2), (1, y1), (3, y3)):
         at = 3 - hop
         meta[at] = [copy(META + at, src, dst.at[at], (peer, s)) for src, dst in fields]
-    for c in z_relayed + z_direct + z_cross + meta[1] + meta[2] + meta[0] + z_mate:
+    @pl.when(sends_ahead)
+    def _():
+        z_held[0].start()
+
+    @pl.when(jnp.logical_not(is_zero))
+    def _():
+        for c in (z_relayed[0], z_direct[0], z_cross[0]):
+            c.start()
+
+    for c in [z_relayed[1], z_direct[1], z_cross[1]] + meta[1] + meta[2] + meta[0] + z_mate:
         c.start()
 
     def weight_of(slot, frac, held):
@@ -142,13 +198,28 @@
     obs_t[...] = jnp.transpose(obs_ref[...])
     inv_t[...] = jnp.transpose(jnp.broadcast_to(inv_ref[...], (chans, chans)))
     arrived(Z_MATE, zbuf.at[HEAD : HEAD + 2, 1])
+
+    @pl.when(sends_ahead)
+    def _():
+        z_held[1].start()
+
     centre(0)
+    @pl.when(is_keeper)
+    def _():
+        pl.semaphore_wait(barrier, 7)
+        arrived(HELD, held)
+        for c in z_passed:
+            c.start()
+        for device in ((t, 0), (mate, 0)):
+            pl.semaphore_signal(gate, inc=1, device_id=device, device_id_type=MESH)
+
+    for k in (1, 0):
+        z_relayed[k].wait_recv()
+        z_onward[k].start()
+
     for group in (1, 3):
         gathered(group)
         centre(group)
-    for k in (1, 0):
-        z_relayed[k].wait_recv()
-        z_onward[k].start()
     gathered(2)
     centre(2)
     arrived(Z_REST, zbuf.at[0:3, 0])
@@ -244,10 +315,14 @@
     r_swap = [copy(SWAP + k, wout.at[k, 0, bottom], swap.at[k], (mate, s)) for k, d in ends]
     r_sum = [copy(RIMS, wout.at[k, 1, bottom], rim.at[1 - k, 2], (mate, d)) for k, d in ends]
     r_mate = [copy(RIMS, wout.at[2 + k, 1], win.at[k], (mate, s)) for k in range(2)]
-    last = ((2, (2, 3)),)
-    v = by_slot(last)
-    for k in (LEFT, RIGHT):
-        total = wide[k] + sums(v, last, k)
+    @pl.when(is_zero)
+    def _():
+        pl.semaphore_wait(gate, 1)
+
+    final = ((2, (2, 3)),)
+    v = by_slot(final)
+    for k in (RIGHT, LEFT):
+        total = wide[k] + sums(v, final, k)
         wide[k] = total
         wout[k, 0] = total[:chans].astype(BF16)
         wout[k, 1, 0:64] = total[chans : chans + 64].astype(BF16)
@@ -255,11 +330,11 @@
         r_own[k].start()
         r_other[k].start()
     for k in range(2):
-        total = wide[HEAD + k] + sums(v, last, HEAD + k)
+        total = wide[HEAD + k] + sums(v, final, HEAD + k)
         wide[HEAD + k] = total
         wout[2 + k, 1] = total[chans:].astype(BF16)
         r_mate[k].start()
-    for k in (LEFT, RIGHT):
+    for k in (RIGHT, LEFT):
         r_swap[k].wait_recv()
         wout[k, 1, 64:128] = (wide[k, chans + 64 : 2 * chans] + swap[k].astype(F32)).astype(BF16)
         r_sum[k].start()
@@ -268,8 +343,22 @@
         rims = jnp.concatenate([rim[h, 0].astype(F32) + rim[h, 1].astype(F32), rim[h, 2].astype(F32)], axis=0)
         whole = wide[HEAD + h, 0:chans] + win[h].astype(F32) + rims
         adj_out[:, 0, h * 256 : (h + 1) * 256] = jnp.dot(jac_ref[...], whole.astype(BF16), preferred_element_type=F32)
-    sent = foot.at[0:3, 0:528]
-    copy(META, sent, sent, (mate, s)).wait_send()
+    def left_here(ref, out):
+        copy(META, ref, ref, (mate, s), out).wait_send()
+
+    left_here(foot.at[0:3, 0:496], 0)
+
+    @pl.when(sends_ahead)
+    def _():
+        left_here(held, 1)
+
+    @pl.when(jnp.logical_not(is_zero))
+    def _():
+        left_here(foot.at[0:3, 0:32], 1)
+
+    @pl.when(is_keeper)
+    def _():
+        left_here(foot.at[0:3, 0:64], 2)
 
 
 def write(dep_in, adj_in, dep_out, adj_out, done):
@@ -287,7 +376,7 @@
     vmem = pl.BlockSpec(memory_space=pltpu.VMEM)
     i32 = jnp.int32
     departures, adjoint = pl.pallas_call(
-        functools.partial(kernel, n_space, 512 * n_space),
+        functools.partial(kernel, n_space, 512 * n_space, 3 if n_space > 4 else 2),
         out_shape=(
             pltpu.VMEM((512, 128), F32),
             pltpu.VMEM((levels, 1, 512), F32),
@@ -306,6 +395,7 @@
             pltpu.VMEM((4, 1, 512), F32),
             pltpu.VMEM((3, 4, 1, 512), F32),
             pltpu.VMEM((3, 8, 512), BF16),
+            pltpu.VMEM((2, 128, 256), BF16),
             pltpu.VMEM((4, 1024, 512), BF16),
             pltpu.VMEM((4, 2, 128, 256), BF16),
             pltpu.VMEM((4, 256, 512), F32),
@@ -323,8 +413,9 @@
             pltpu.VMEM((128, 128), F32),
             pltpu.VMEM((128, 512), F32),
             pltpu.SemaphoreType.DMA((8,)),
-            pltpu.SemaphoreType.DMA((1,)),
+            pltpu.SemaphoreType.DMA((3,)),
             pltpu.SemaphoreType.DMA((ARRIVALS,)),
+            pltpu.SemaphoreType.REGULAR,
         ],
         compiler_params=pltpu.CompilerParams(collective_id=0, has_side_effects=True),
         name="window",

time: 38.7 us -> 37.7 us (0.974)
  Pallas kernels: 37.3 us -> 36.3 us
    pallas_call x1, Pallas kernels: 36.5 us -> 35.5 us  [body(): pl.pallas_call(functools.partial(kernel, n_space, 512 * n_space, 3 if n_s...]
where the time goes in v5:
time: 37.7 us; the launch traced here: 37.6 us
  Pallas kernels  36.3 us (96%)
  between operations  1.29 us (3%)
    pallas_call x1, Pallas kernels, body(): pl.pallas_call(functools.partial(kernel, n_space, 512 * n_space, 3 if n_s...  35.5 us
    pallas_call x1, Pallas kernels, body(): pl.pallas_call(write, out_shape=(jax.ShapeDtypeStruct(departures.shape, F...  0.81 us

profile of v5, /device:TPU:1, one launch (start us, length us, event | category | flops | bytes accessed | tf_op | source)
XLA Modules:
  0.0 37.6 jit_solution(1913992538273181907)
XLA Ops:
  1.3 35.5 %window.1 = (f32[512,128]{1,0:T(8,128)S(1)}, f32[137,1,512]{2,1,0:T(1,128)S(1)}) custom-call(bf16[137,512]{1,0:T(8,128)(2,1)} %bitcast.9, s32[1,512]{1,0:T(1,128)} %bitcast.11, bf16[8,512]{1,0:T(8,128)(2,1)} %bitcast.10, s32[1,512]{1,0:T(1,128)} %bitcast.12, f32[1,512]{1,0:T(1,128)} %bitcast.13, s32[1,1]{1,0:T(1,128)S(6)} %copy.11.count_ref, ...), custom_call_target="tpu_custom_call" | custom-call | tf_op jit(solution)/shard_map/window/pallas_call | solution.py:378
  36.8 0.8 %write.1 = (f32[512,128]{1,0:T(8,128)}, f32[137,1,512]{2,1,0:T(1,128)}) custom-call(f32[512,128]{1,0:T(8,128)S(1)} %get-tuple-element.6.dep_in, f32[137,1,512]{2,1,0:T(1,128)S(1)} %get-tuple-element.7.adj_in), custom_call_target="tpu_custom_call" | custom-call | tf_op jit(solution)/shard_map/write/pallas_call | solution.py:433

commit v6 on v5

--- a/solution.py
+++ b/solution.py
@@ -12,7 +12,7 @@
 BF16 = jnp.bfloat16
 
 META, Z_MATE, Z_RELAYED, Z_REST, FAR, SUM, FIRST, SECOND, LAST, SWAP, RIMS, HELD = 0, 3, 4, 6, 7, 11, 15, 19, 20, 22, 24, 25
-ARRIVALS = 26
+ARRIVALS = 27
 
 LEFT, RIGHT, HEAD, TAIL = 0, 1, 2, 3
 
@@ -122,7 +122,10 @@
     z_cross = [copy(Z_REST, zbuf.at[a, 0, bottom], zbuf.at[b, 1, bottom], (mate, d), 1 - k) for k, (a, b, d) in enumerate(sides)]
     z_onward = [copy(Z_REST, zbuf.at[b, 0, top], zbuf.at[b, 1, top], (mate, s)) for a, b, d in sides]
     z_mate = [copy(Z_MATE, zbuf.at[a, 0], zbuf.at[a, 1], (mate, s)) for a, b, d in sides]
-    z_held = [copy(HELD, zbuf.at[HEAD, k], held.at[k], (t, holder), 1) for k in range(2)]
+    z_held = [
+        [copy(HELD + j, zbuf.at[HEAD, 0, rows], held.at[1 - k, rows], (second_core, holder), 1) for j, rows in ((0, top), (1, bottom))]
+        for k in range(2)
+    ]
     last = n_space - 1
     z_passed = [
         copy(Z_RELAYED, held.at[1, top], zbuf.at[RIGHT, 0, top], (mate, last), 2),
@@ -132,15 +135,17 @@
         copy(Z_REST, held.at[0, bottom], zbuf.at[RIGHT, 0, bottom], (t, last), 2),
         copy(Z_REST, held.at[1, bottom], zbuf.at[RIGHT, 1, bottom], (t, last), 2),
     ]
-    sends_ahead = jnp.logical_and(is_zero, core == 1)
     fields = ((o_pack, m_pack), (w_ref, m_w))
     meta = {}
     for hop, peer in ((2, y2), (1, y1), (3, y3)):
         at = 3 - hop
         meta[at] = [copy(META + at, src, dst.at[at], (peer, s)) for src, dst in fields]
-    @pl.when(sends_ahead)
-    def _():
-        z_held[0].start()
+    for k in range(2):
+
+        @pl.when(jnp.logical_and(is_zero, core == k))
+        def _():
+            for c in z_held[k]:
+                c.start()
 
     @pl.when(jnp.logical_not(is_zero))
     def _():
@@ -198,25 +203,23 @@
     obs_t[...] = jnp.transpose(obs_ref[...])
     inv_t[...] = jnp.transpose(jnp.broadcast_to(inv_ref[...], (chans, chans)))
     arrived(Z_MATE, zbuf.at[HEAD : HEAD + 2, 1])
-
-    @pl.when(sends_ahead)
-    def _():
-        z_held[1].start()
-
     centre(0)
     @pl.when(is_keeper)
     def _():
         pl.semaphore_wait(barrier, 7)
-        arrived(HELD, held)
-        for c in z_passed:
+        arrived(HELD, held.at[:, top])
+        for c in z_passed[:2]:
+            c.start()
+        arrived(HELD + 1, held.at[:, bottom])
+        for c in z_passed[2:]:
             c.start()
         for device in ((t, 0), (mate, 0)):
             pl.semaphore_signal(gate, inc=1, device_id=device, device_id_type=MESH)
 
-    for k in (1, 0):
-        z_relayed[k].wait_recv()
-        z_onward[k].start()
-
+    z_relayed[1].wait_recv()
+    z_onward[1].start()
+    z_relayed[0].wait_recv()
+    z_onward[0].start()
     for group in (1, 3):
         gathered(group)
         centre(group)
@@ -327,17 +330,35 @@
         wout[k, 0] = total[:chans].astype(BF16)
         wout[k, 1, 0:64] = total[chans : chans + 64].astype(BF16)
         r_swap[k].start()
-        r_own[k].start()
-        r_other[k].start()
+
+        @pl.when(core == 0)
+        def _():
+            r_other[k].start()
+
+        @pl.when(core == 1)
+        def _():
+            r_own[k].start()
+
+    for k in (RIGHT, LEFT):
+        r_swap[k].wait_recv()
+        wout[k, 1, 64:128] = (wide[k, chans + 64 : 2 * chans] + swap[k].astype(F32)).astype(BF16)
+        r_sum[k].start()
+
+    @pl.when(core == 0)
+    def _():
+        for k in (RIGHT, LEFT):
+            r_own[k].start()
+
+    @pl.when(core == 1)
+    def _():
+        for k in (RIGHT, LEFT):
+            r_other[k].start()
+
     for k in range(2):
         total = wide[HEAD + k] + sums(v, final, HEAD + k)
         wide[HEAD + k] = total
         wout[2 + k, 1] = total[chans:].astype(BF16)
         r_mate[k].start()
-    for k in (RIGHT, LEFT):
-        r_swap[k].wait_recv()
-        wout[k, 1, 64:128] = (wide[k, chans + 64 : 2 * chans] + swap[k].astype(F32)).astype(BF16)
-        r_sum[k].start()
     arrived(RIMS, pout.at[0:10])
     for h in range(2):
         rims = jnp.concatenate([rim[h, 0].astype(F32) + rim[h, 1].astype(F32), rim[h, 2].astype(F32)], axis=0)
@@ -348,9 +369,9 @@
 
     left_here(foot.at[0:3, 0:496], 0)
 
-    @pl.when(sends_ahead)
-    def _():
-        left_here(held, 1)
+    @pl.when(is_zero)
+    def _():
+        left_here(held.at[0], 1)
 
     @pl.when(jnp.logical_not(is_zero))
     def _():

time: 37.7 us -> 36.9 us (0.979)
  Pallas kernels: 36.3 us -> 35.5 us
    pallas_call x1, Pallas kernels: 35.5 us -> 34.7 us  [body(): pl.pallas_call(functools.partial(kernel, n_space, 512 * n_space, 3 if n_s...]
where the time goes in v6:
time: 36.9 us; the launch traced here: 36.8 us
  Pallas kernels  35.5 us (96%)
  between operations  1.29 us (3%)
    pallas_call x1, Pallas kernels, body(): pl.pallas_call(functools.partial(kernel, n_space, 512 * n_space, 3 if n_s...  34.7 us
    pallas_call x1, Pallas kernels, body(): pl.pallas_call(write, out_shape=(jax.ShapeDtypeStruct(departures.shape, F...  0.81 us

profile of v6, /device:TPU:1, one launch (start us, length us, event | category | flops | bytes accessed | tf_op | source)
XLA Modules:
  0.0 36.8 jit_solution(14522145893473227129)
XLA Ops:
  1.3 34.7 %window.1 = (f32[512,128]{1,0:T(8,128)S(1)}, f32[137,1,512]{2,1,0:T(1,128)S(1)}) custom-call(bf16[137,512]{1,0:T(8,128)(2,1)} %bitcast.9, s32[1,512]{1,0:T(1,128)} %bitcast.11, bf16[8,512]{1,0:T(8,128)(2,1)} %bitcast.10, s32[1,512]{1,0:T(1,128)} %bitcast.12, f32[1,512]{1,0:T(1,128)} %bitcast.13, s32[1,1]{1,0:T(1,128)S(6)} %copy.11.count_ref, ...), custom_call_target="tpu_custom_call" | custom-call | tf_op jit(solution)/shard_map/window/pallas_call | solution.py:399
  36.0 0.8 %write.1 = (f32[512,128]{1,0:T(8,128)}, f32[137,1,512]{2,1,0:T(1,128)}) custom-call(f32[512,128]{1,0:T(8,128)S(1)} %get-tuple-element.6.dep_in, f32[137,1,512]{2,1,0:T(1,128)S(1)} %get-tuple-element.7.adj_in), custom_call_target="tpu_custom_call" | custom-call | tf_op jit(solution)/shard_map/write/pallas_call | solution.py:454

commit v7 on v6

--- a/solution.py
+++ b/solution.py
@@ -11,8 +11,8 @@
 F32 = jnp.float32
 BF16 = jnp.bfloat16
 
-META, Z_MATE, Z_RELAYED, Z_REST, FAR, SUM, FIRST, SECOND, LAST, SWAP, RIMS, HELD = 0, 3, 4, 6, 7, 11, 15, 19, 20, 22, 24, 25
-ARRIVALS = 27
+META, Z_MATE, Z_RELAYED, Z_REST, FAR, SUM, FIRST, SECOND, LAST, SWAP, RIMS, W_MATE, HELD = 0, 3, 4, 6, 7, 11, 15, 19, 20, 22, 24, 26, 27
+ARRIVALS = 29
 
 LEFT, RIGHT, HEAD, TAIL = 0, 1, 2, 3
 
@@ -147,7 +147,9 @@
             for c in z_held[k]:
                 c.start()
 
-    @pl.when(jnp.logical_not(is_zero))
+    gives_way = s == holder + 1
+
+    @pl.when(jnp.logical_not(jnp.logical_or(is_zero, gives_way)))
     def _():
         for c in (z_relayed[0], z_direct[0], z_cross[0]):
             c.start()
@@ -203,6 +205,12 @@
     obs_t[...] = jnp.transpose(obs_ref[...])
     inv_t[...] = jnp.transpose(jnp.broadcast_to(inv_ref[...], (chans, chans)))
     arrived(Z_MATE, zbuf.at[HEAD : HEAD + 2, 1])
+
+    @pl.when(gives_way)
+    def _():
+        for c in (z_relayed[0], z_direct[0], z_cross[0]):
+            c.start()
+
     centre(0)
     @pl.when(is_keeper)
     def _():
@@ -313,11 +321,11 @@
     spread((2, (0, 1)))
     arrived(LAST + 1, sbuf.at[2, 2:4])
     ends = ((LEFT, left), (RIGHT, right))
-    r_own = [copy(RIMS, wout.at[k, 0, top], rim.at[1 - k, 0], (t, d)) for k, d in ends]
-    r_other = [copy(RIMS, wout.at[k, 1, top], rim.at[1 - k, 1], (mate, d)) for k, d in ends]
+    r_own = [copy(RIMS + k, wout.at[k, 0, top], rim.at[1 - k, 0], (t, d)) for k, d in ends]
+    r_other = [copy(RIMS + k, wout.at[k, 1, top], rim.at[1 - k, 1], (mate, d)) for k, d in ends]
     r_swap = [copy(SWAP + k, wout.at[k, 0, bottom], swap.at[k], (mate, s)) for k, d in ends]
-    r_sum = [copy(RIMS, wout.at[k, 1, bottom], rim.at[1 - k, 2], (mate, d)) for k, d in ends]
-    r_mate = [copy(RIMS, wout.at[2 + k, 1], win.at[k], (mate, s)) for k in range(2)]
+    r_sum = [copy(RIMS + k, wout.at[k, 1, bottom], rim.at[1 - k, 2], (mate, d)) for k, d in ends]
+    r_mate = [copy(W_MATE, wout.at[2 + k, 1], win.at[k], (mate, s)) for k in range(2)]
     @pl.when(is_zero)
     def _():
         pl.semaphore_wait(gate, 1)
@@ -359,8 +367,9 @@
         wide[HEAD + k] = total
         wout[2 + k, 1] = total[chans:].astype(BF16)
         r_mate[k].start()
-    arrived(RIMS, pout.at[0:10])
-    for h in range(2):
+    arrived(W_MATE, win)
+    for h in (1, 0):
+        arrived(RIMS + 1 - h, rim.at[h])
         rims = jnp.concatenate([rim[h, 0].astype(F32) + rim[h, 1].astype(F32), rim[h, 2].astype(F32)], axis=0)
         whole = wide[HEAD + h, 0:chans] + win[h].astype(F32) + rims
         adj_out[:, 0, h * 256 : (h + 1) * 256] = jnp.dot(jac_ref[...], whole.astype(BF16), preferred_element_type=F32)

time: 36.9 us -> 36 us (0.976)
  Pallas kernels: 35.5 us -> 34.6 us
    pallas_call x1, Pallas kernels: 34.7 us -> 33.8 us  [body(): pl.pallas_call(functools.partial(kernel, n_space, 512 * n_space, 3 if n_s...]
where the time goes in v7:
time: 36 us; the launch traced here: 35.9 us
  Pallas kernels  34.6 us (96%)
  between operations  1.29 us (4%)
    pallas_call x1, Pallas kernels, body(): pl.pallas_call(functools.partial(kernel, n_space, 512 * n_space, 3 if n_s...  33.8 us
    pallas_call x1, Pallas kernels, body(): pl.pallas_call(write, out_shape=(jax.ShapeDtypeStruct(departures.shape, F...  0.81 us

profile of v7, /device:TPU:1, one launch (start us, length us, event | category | flops | bytes accessed | tf_op | source)
XLA Modules:
  0.0 35.9 jit_solution(7630318748426300758)
XLA Ops:
  1.3 33.8 %window.1 = (f32[512,128]{1,0:T(8,128)S(1)}, f32[137,1,512]{2,1,0:T(1,128)S(1)}) custom-call(bf16[137,512]{1,0:T(8,128)(2,1)} %bitcast.9, s32[1,512]{1,0:T(1,128)} %bitcast.11, bf16[8,512]{1,0:T(8,128)(2,1)} %bitcast.10, s32[1,512]{1,0:T(1,128)} %bitcast.12, f32[1,512]{1,0:T(1,128)} %bitcast.13, s32[1,1]{1,0:T(1,128)S(6)} %copy.11.count_ref, ...), custom_call_target="tpu_custom_call" | custom-call | tf_op jit(solution)/shard_map/window/pallas_call | solution.py:408
  35.1 0.8 %write.1 = (f32[512,128]{1,0:T(8,128)}, f32[137,1,512]{2,1,0:T(1,128)}) custom-call(f32[512,128]{1,0:T(8,128)S(1)} %get-tuple-element.6.dep_in, f32[137,1,512]{2,1,0:T(1,128)S(1)} %get-tuple-element.7.adj_in), custom_call_target="tpu_custom_call" | custom-call | tf_op jit(solution)/shard_map/write/pallas_call | solution.py:463

commit v8 on v7

--- a/solution.py
+++ b/solution.py
@@ -211,7 +211,6 @@
         for c in (z_relayed[0], z_direct[0], z_cross[0]):
             c.start()
 
-    centre(0)
     @pl.when(is_keeper)
     def _():
         pl.semaphore_wait(barrier, 7)
@@ -228,16 +227,20 @@
     z_onward[1].start()
     z_relayed[0].wait_recv()
     z_onward[0].start()
-    for group in (1, 3):
+    for group in (3,):
+        gathered(group)
+    for group in (2,):
         gathered(group)
         centre(group)
-    gathered(2)
-    centre(2)
+    gathered(1)
     arrived(Z_REST, zbuf.at[0:3, 0])
 
-    def finish(group):
-        total = acc[group] + jnp.dot(columns(LEFT), foot[group, 0:512, :], preferred_element_type=F32)
+    def weighted(group, total):
         return abuf[group, 0:1, :] * total[:chans] + abuf[group, 1:2, :] * total[chans:]
+
+    def partials(group):
+        whole = jnp.concatenate([columns(LEFT), columns(HEAD)], axis=1)
+        return weighted(group, jnp.dot(whole, foot[group], preferred_element_type=F32))
 
     def lanes(q):
         return slice(q * quarter, (q + 1) * quarter)
@@ -245,18 +248,18 @@
     far = [copy(FAR + q, pout.at[q], relay.at[q], ((y1, y3)[q % 2], s)) for q in range(4)]
     to_next = [copy(SUM + q, pout.at[4 + q], rin.at[0, q], (y1, s)) for q in range(4)]
     to_last = [copy(SUM + q, pout.at[8 + q], rin.at[1, q], (y3, s)) for q in range(4)]
-    partial = finish(2)
+    partial = weighted(2, acc[2] + jnp.dot(columns(LEFT), foot[2, 0:512, :], preferred_element_type=F32))
     for q in range(4):
         pout[q] = partial[:, lanes(q)].astype(BF16)
         far[q].start()
     for group, base, copies, now in ((1, 4, to_next, 1), (3, 8, to_last, 0)):
-        partial = finish(group)
+        partial = partials(group)
         for q in (now, now + 2):
             pout[base + q] = partial[:, lanes(q)].astype(BF16)
             copies[q].start()
         for q in (1 - now, 3 - now):
             acc[group, 0:chans, lanes(q)] = partial[:, lanes(q)]
-    acc[0, 0:chans] = finish(0)
+    acc[0, 0:chans] = partials(0)
     for q in range(4):
         group, base, copies = ((1, 4, to_next), (3, 8, to_last))[q % 2]
         far[q].wait_recv()

time: 36 us -> 35.5 us (0.986)
  Pallas kernels: 34.6 us -> 34.1 us
    pallas_call x1, Pallas kernels: 33.8 us -> 33.3 us  [body(): pl.pallas_call(functools.partial(kernel, n_space, 512 * n_space, 3 if n_s...]
where the time goes in v8:
time: 35.5 us; the launch traced here: 35.4 us
  Pallas kernels  34.1 us (96%)
  between operations  1.29 us (4%)
    pallas_call x1, Pallas kernels, body(): pl.pallas_call(functools.partial(kernel, n_space, 512 * n_space, 3 if n_s...  33.3 us
    pallas_call x1, Pallas kernels, body(): pl.pallas_call(write, out_shape=(jax.ShapeDtypeStruct(departures.shape, F...  0.81 us

profile of v8, /device:TPU:1, one launch (start us, length us, event | category | flops | bytes accessed | tf_op | source)
XLA Modules:
  0.0 35.4 jit_solution(13107386792150758014)
XLA Ops:
  1.3 33.3 %window.1 = (f32[512,128]{1,0:T(8,128)S(1)}, f32[137,1,512]{2,1,0:T(1,128)S(1)}) custom-call(bf16[137,512]{1,0:T(8,128)(2,1)} %bitcast.9, s32[1,512]{1,0:T(1,128)} %bitcast.11, bf16[8,512]{1,0:T(8,128)(2,1)} %bitcast.10, s32[1,512]{1,0:T(1,128)} %bitcast.12, f32[1,512]{1,0:T(1,128)} %bitcast.13, s32[1,1]{1,0:T(1,128)S(6)} %copy.11.count_ref, ...), custom_call_target="tpu_custom_call" | custom-call | tf_op jit(solution)/shard_map/window/pallas_call | solution.py:411
  34.6 0.8 %write.1 = (f32[512,128]{1,0:T(8,128)}, f32[137,1,512]{2,1,0:T(1,128)}) custom-call(f32[512,128]{1,0:T(8,128)S(1)} %get-tuple-element.6.dep_in, f32[137,1,512]{2,1,0:T(1,128)S(1)} %get-tuple-element.7.adj_in), custom_call_target="tpu_custom_call" | custom-call | tf_op jit(solution)/shard_map/write/pallas_call | solution.py:466

commit v9 on v8

--- a/solution.py
+++ b/solution.py
@@ -140,6 +140,9 @@
     for hop, peer in ((2, y2), (1, y1), (3, y3)):
         at = 3 - hop
         meta[at] = [copy(META + at, src, dst.at[at], (peer, s)) for src, dst in fields]
+    for c in meta[1]:
+        c.start()
+
     for k in range(2):
 
         @pl.when(jnp.logical_and(is_zero, core == k))
@@ -154,7 +157,7 @@
         for c in (z_relayed[0], z_direct[0], z_cross[0]):
             c.start()
 
-    for c in [z_relayed[1], z_direct[1], z_cross[1]] + meta[1] + meta[2] + meta[0] + z_mate:
+    for c in [z_relayed[1], z_direct[1], z_cross[1]] + meta[2] + meta[0] + z_mate:
         c.start()
 
     def weight_of(slot, frac, held):

time: 35.5 us -> 35.5 us (level)
  no operation moved by 1% of the time
where the time goes in v9:
time: 35.5 us; the launch traced here: 35.4 us
  Pallas kernels  34.1 us (96%)
  between operations  1.29 us (4%)
    pallas_call x1, Pallas kernels, body(): pl.pallas_call(functools.partial(kernel, n_space, 512 * n_space, 3 if n_s...  33.3 us
    pallas_call x1, Pallas kernels, body(): pl.pallas_call(write, out_shape=(jax.ShapeDtypeStruct(departures.shape, F...  0.81 us

profile of v9, /device:TPU:1, one launch (start us, length us, event | category | flops | bytes accessed | tf_op | source)
XLA Modules:
  0.0 35.4 jit_solution(6135611500222481396)
XLA Ops:
  1.3 33.3 %window.1 = (f32[512,128]{1,0:T(8,128)S(1)}, f32[137,1,512]{2,1,0:T(1,128)S(1)}) custom-call(bf16[137,512]{1,0:T(8,128)(2,1)} %bitcast.9, s32[1,512]{1,0:T(1,128)} %bitcast.11, bf16[8,512]{1,0:T(8,128)(2,1)} %bitcast.10, s32[1,512]{1,0:T(1,128)} %bitcast.12, f32[1,512]{1,0:T(1,128)} %bitcast.13, s32[1,1]{1,0:T(1,128)S(6)} %copy.11.count_ref, ...), custom_call_target="tpu_custom_call" | custom-call | tf_op jit(solution)/shard_map/window/pallas_call | solution.py:414
  34.6 0.8 %write.1 = (f32[512,128]{1,0:T(8,128)}, f32[137,1,512]{2,1,0:T(1,128)}) custom-call(f32[512,128]{1,0:T(8,128)S(1)} %get-tuple-element.6.dep_in, f32[137,1,512]{2,1,0:T(1,128)S(1)} %get-tuple-element.7.adj_in), custom_call_target="tpu_custom_call" | custom-call | tf_op jit(solution)/shard_map/write/pallas_call | solution.py:469

commit v10 on v9

--- a/solution.py
+++ b/solution.py
@@ -140,7 +140,7 @@
     for hop, peer in ((2, y2), (1, y1), (3, y3)):
         at = 3 - hop
         meta[at] = [copy(META + at, src, dst.at[at], (peer, s)) for src, dst in fields]
-    for c in meta[1]:
+    for c in meta[1] + meta[2] + meta[0]:
         c.start()
 
     for k in range(2):
@@ -157,7 +157,7 @@
         for c in (z_relayed[0], z_direct[0], z_cross[0]):
             c.start()
 
-    for c in [z_relayed[1], z_direct[1], z_cross[1]] + meta[2] + meta[0] + z_mate:
+    for c in [z_relayed[1], z_direct[1], z_cross[1]] + z_mate:
         c.start()
 
     def weight_of(slot, frac, held):

time: 35.5 us -> 35.5 us (level)
  no operation moved by 1% of the time
where the time goes in v10:
time: 35.5 us; the launch traced here: 35.4 us
  Pallas kernels  34.1 us (96%)
  between operations  1.29 us (4%)
    pallas_call x1, Pallas kernels, body(): pl.pallas_call(functools.partial(kernel, n_space, 512 * n_space, 3 if n_s...  33.3 us
    pallas_call x1, Pallas kernels, body(): pl.pallas_call(write, out_shape=(jax.ShapeDtypeStruct(departures.shape, F...  0.81 us

profile of v10, /device:TPU:1, one launch (start us, length us, event | category | flops | bytes accessed | tf_op | source)
XLA Modules:
  0.0 35.4 jit_solution(486046571525817894)
XLA Ops:
  1.3 33.3 %window.1 = (f32[512,128]{1,0:T(8,128)S(1)}, f32[137,1,512]{2,1,0:T(1,128)S(1)}) custom-call(bf16[137,512]{1,0:T(8,128)(2,1)} %bitcast.9, s32[1,512]{1,0:T(1,128)} %bitcast.11, bf16[8,512]{1,0:T(8,128)(2,1)} %bitcast.10, s32[1,512]{1,0:T(1,128)} %bitcast.12, f32[1,512]{1,0:T(1,128)} %bitcast.13, s32[1,1]{1,0:T(1,128)S(6)} %copy.11.count_ref, ...), custom_call_target="tpu_custom_call" | custom-call | tf_op jit(solution)/shard_map/window/pallas_call | solution.py:414
  34.6 0.8 %write.1 = (f32[512,128]{1,0:T(8,128)}, f32[137,1,512]{2,1,0:T(1,128)}) custom-call(f32[512,128]{1,0:T(8,128)S(1)} %get-tuple-element.6.dep_in, f32[137,1,512]{2,1,0:T(1,128)S(1)} %get-tuple-element.7.adj_in), custom_call_target="tpu_custom_call" | custom-call | tf_op jit(solution)/shard_map/write/pallas_call | solution.py:469
